TPU v7x, 128 devices: a whole 4x4x4 slice. The times are simulated.
128 devices in a mesh: section: 8 (over y, core), sim: 16 (over z, x).
Axes of the slice: x: 4, y: 4, z: 4, core: 2. Of those that a mesh axis runs over, the one named last changes fastest.
Arguments:
- state: float32 [256, 64, 16384], P('section', None, 'sim'), may hold values from -60 to 60
- owner: int32 [256, 1], P('section'), may hold values from 0 to 15; in each aligned block of 32 rows (0 to 31, 32 to 63, ...) at most 4 rows name the same one
- counts: int32 [256], P('section'), may hold values from 4096 to 16384
Outputs:
- slab_mean: float32 [256, 64], P('section')
- slab_cov: float32 [256, 4096], P('section', 'sim')
- group_cov: float32 [128, 4096], P(('section', 'sim'))
- global_mean: float32 [64], replicated
- global_cov: float32 [64, 64], replicated
Inputs may be any that keep to these rules, and one draw needn't show every extreme that they name: Among the 32 slabs of one group, no owner is named by more than 4 slabs, and one owner is named by exactly 4 slabs in some or all groups.
All inputs are finite; a program needn't handle non-finite values.
Results may differ from a plain program's by a relative error of at most 0.0003.
Values sent between devices are 32-bit elements; how exact they have to be, the bound alone decides.
No kernel may reach another device: no remote copies, remote signals or barrier semaphores. Data moves between devices by JAX's collectives and lax.ppermute only.
A program may use at most 64 MiB of HBM per device.

v0:
```python
import jax
import jax.numpy as jnp
from jax import lax
from jax.sharding import Mesh
from jax.sharding import PartitionSpec as P

SIM = ("sim_0", "sim_1")
SECTION_SIM = ("section_0", "section_1", "sim_0", "sim_1")
SECTION = ("section_0", "section_1")


def sent_to_all(value, axis):
    count = lax.axis_size(axis)
    return lax.all_to_all(
        jnp.broadcast_to(value[None], (count, *value.shape)), axis, 0, 0, tiled=True
    )


def taken_together(value, axis):
    return sent_to_all(value, axis).sum(axis=0)


def split_up(value, dim, count):
    before, after = (value.shape[:dim], value.shape[dim + 1 :])
    return jnp.moveaxis(value.reshape(*before, count, -1, *after), dim, 0)


def sum_at_owner(value, axis, dim):
    count = lax.axis_size(axis)
    pieces = lax.all_to_all(split_up(value, dim, count), axis, 0, 0, tiled=True)
    return jnp.sum(pieces, axis=0)


def by_axis(value, axes):
    far, near = axes
    return taken_together(taken_together(value, near), far)


def together(arrays, axis):
    ends = [0]
    for a in arrays:
        ends.append(ends[-1] + a.size)
    running = by_axis(jnp.concatenate([a.ravel() for a in arrays]), axis)
    return tuple((running[b:e].reshape(a.shape) for a, b, e in zip(arrays, ends, ends[1:])))


def local(state, owner, counts):
    high = lax.Precision.HIGHEST
    slab_here, width, cells_dev = state.shape
    n_sim = lax.axis_size(SIM)
    my_index = lax.axis_index(SIM)
    target = owner[:, 0]
    totals = counts.astype(jnp.float32)
    tile_start = my_index * cells_dev
    live = jnp.arange(cells_dev, dtype=jnp.int32)[None, :] + tile_start < counts[:, None]
    tile_sum = jnp.sum(jnp.where(live[:, None, :], state, 0.0), axis=2)
    slab_sum = taken_together(tile_sum, SIM)
    slab_mean = slab_sum / totals[:, None]
    centered = jnp.where(live[:, None, :], state - slab_mean[:, :, None], 0.0)
    tile_co = jnp.einsum("svc,swc->svw", centered, centered, precision=high).reshape(
        slab_here, width * width
    )
    slab_part = sum_at_owner(tile_co, SIM, 1)
    slab_cov = slab_part / (totals - 1.0)[:, None]
    member = (target[:, None] == jnp.arange(n_sim, dtype=jnp.int32)[None, :]).astype(jnp.float32)
    owner_terms = jnp.dot(member.T, tile_co, precision=high)
    own_terms = sum_at_owner(owner_terms, SIM, 0)[0]
    weight = jnp.where(target == my_index, totals, 0.0)
    group_count = jnp.sum(weight)
    group_mean = jnp.sum(weight[:, None] * slab_mean, axis=0) / jnp.maximum(group_count, 1.0)
    offset = slab_mean - group_mean[None, :]
    group_co = own_terms + jnp.einsum(
        "k,kv,kw->vw", weight, offset, offset, precision=high
    ).reshape(width * width)
    group_cov = (group_co / jnp.maximum(group_count - 1.0, 1.0))[None, :]
    total, weighted = together(
        (group_count, group_count * group_mean), ("section_0", ("section_1", "sim_0", "sim_1"))
    )
    global_mean = weighted / total
    gap = group_mean - global_mean
    spread = by_axis(
        group_co + group_count * jnp.outer(gap, gap).reshape(-1),
        (("section_0", "section_1"), ("sim_0", "sim_1")),
    )
    global_cov = (spread / (total - 1.0)).reshape(width, width)
    return (slab_mean, slab_cov, group_cov, global_mean, global_cov)


def solution(mesh):
    finer = Mesh(mesh.devices.reshape(4, 2, 4, 4), ("section_0", "section_1", "sim_0", "sim_1"))
    return jax.shard_map(
        local,
        mesh=finer,
        in_specs=(P(SECTION, None, SIM), P(SECTION, None), P(SECTION)),
        out_specs=(P(SECTION, None), P(SECTION, SIM), P(SECTION_SIM, None), P(), P()),
        check_vma=False,
    )
```

profile of v0, /device:TPU:0, one launch (start us, length us, event | category | flops | bytes accessed | tf_op | source)
XLA Modules:
  0.0 109.5 jit_solution(13462422381912311473)
XLA Ops:
  0.6 0.0 copy-start.1
  0.6 0.0 copy-start.2
  0.7 0.8 broadcast_compare_fusion
  1.5 4.1 %select_reduce_fusion = f32[32,64]{1,0:T(8,128)S(1)} fusion(f32[32,64,1024]{2,1,0:T(8,128)} %param.3, pred[32,1024]{1,0:T(8,128)(4,1)S(1)} %broadcast_compare_fusion), kind=kLoop, calls=%fused_computation.3 | loop fusion | flops 4192256 | bytes 8429568 | tf_op jit(solution)/shard_map/reduce_sum | solution.py:56
  5.6 0.8 reshape.152
  6.4 8.0 %all-to-all-start = ((f32[16,1,2048]{2,1,0:T(1,128)}), f32[16,1,2048]{2,1,0:T(1,128)S(1)}, u32[]{:S(2)}, u32[]{:S(2)}) async-start(f32[16,1,2048]{2,1,0:T(1,128)} %reshape.152), calls=%async_computation | async-start | bytes 262144 | tf_op jit(solution)/shard_map/all_to_all | solution.py:14
  14.4 0.0 copy-done.1
  14.4 0.0 copy-done.2
  14.4 0.6 fusion.14
  15.7 6.7 %all-to-all-done = f32[16,1,2048]{2,1,0:T(1,128)S(1)} async-done(((f32[16,1,2048]{2,1,0:T(1,128)}), f32[16,1,2048]{2,1,0:T(1,128)S(1)}, u32[]{:S(2)}, u32[]{:S(2)}) %all-to-all-start) | async-done | bytes 131104 | tf_op jit(solution)/shard_map/all_to_all | solution.py:14
  22.4 0.5 broadcast.79
  22.9 0.9 reduce.5
  23.9 0.1 reshape.153
  24.0 0.1 multiply_reduce_fusion
  24.1 0.0 copy-start
  24.1 0.7 broadcast_multiply_fusion
  24.8 0.7 pad_maximum_fusion
  25.5 0.6 broadcast_in_dim.34
  26.1 3.8 %all-to-all-start.3 = ((f32[32,1,65]{2,1,0:T(1,128)}), f32[32,1,65]{2,1,0:T(1,128)S(1)}, u32[]{:S(2)}, u32[]{:S(2)}) async-start(f32[32,1,65]{2,1,0:T(1,128)} %broadcast_in_dim.34), calls=%async_computation.3 | async-start | bytes 32768 | tf_op jit(solution)/shard_map/all_to_all | solution.py:14
  30.0 14.9 %fusion = f32[32,64,64]{2,1,0:T(8,128)S(1)} fusion(f32[32,64,1024]{2,1,0:T(8,128)} %param.3, f32[32,64]{1,0:T(8,128)S(1)} %get-tuple-element.12, pred[32,1024]{1,0:T(8,128)(4,1)S(1)} %broadcast_compare_fusion), kind=kOutput, calls=%fused_computation | convolution fusion | flops 1614807040 | bytes 8953856 | tf_op jit(solution)/shard_map/svc,swc->svw/dot_general | solution.py:60
  44.9 0.3 fusion.6
  45.2 0.4 reshape.146
  45.6 0.0 all-to-all-done.3
  45.6 0.6 broadcast_in_dim.35
  46.2 4.5 %all-to-all-start.4 = ((f32[4,1,65]{2,1,0:T(1,128)}), f32[4,1,65]{2,1,0:T(1,128)S(1)}, u32[]{:S(2)}, u32[]{:S(2)}) async-start(f32[4,1,65]{2,1,0:T(1,128)} %broadcast_in_dim.35), calls=%async_computation.4 | async-start | bytes 4096 | tf_op jit(solution)/shard_map/all_to_all | solution.py:14
  50.7 0.4 convolution_bitcast_fusion
  51.0 0.1 reshape.151
  51.1 1.0 copy.13
  52.1 3.8 %all-to-all-done.4 = f32[4,1,65]{2,1,0:T(1,128)S(1)} async-done(((f32[4,1,65]{2,1,0:T(1,128)}), f32[4,1,65]{2,1,0:T(1,128)S(1)}, u32[]{:S(2)}, u32[]{:S(2)}) %all-to-all-start.4) | async-done | bytes 1072 | tf_op jit(solution)/shard_map/all_to_all | solution.py:14
  55.9 7.0 %all-to-all-start.2 = ((f32[16,1,4096]{2,1,0:T(1,128)}), f32[16,1,4096]{2,1,0:T(1,128)S(1)}, u32[]{:S(2)}, u32[]{:S(2)}) async-start(f32[16,1,4096]{2,1,0:T(1,128)} %copy.13), calls=%async_computation.2 | async-start | bytes 524288 | tf_op jit(solution)/shard_map/all_to_all | solution.py:30
  62.9 0.6 fusion.13
  63.5 0.7 multiply_multiply_fusion
  64.3 0.1 mul.60
  64.3 7.3 %all-to-all-done.2 = f32[16,1,4096]{2,1,0:T(1,128)S(1)} async-done(((f32[16,1,4096]{2,1,0:T(1,128)}), f32[16,1,4096]{2,1,0:T(1,128)S(1)}, u32[]{:S(2)}, u32[]{:S(2)}) %all-to-all-start.2) | async-done | bytes 262176 | tf_op jit(solution)/shard_map/all_to_all | solution.py:30
  71.6 0.2 reduce_sum.95
  71.8 0.9 broadcast_in_dim.36
  72.7 3.5 %all-to-all-start.5 = ((f32[16,1,4096]{2,1,0:T(1,128)}), f32[16,1,4096]{2,1,0:T(1,128)S(1)}, u32[]{:S(2)}, u32[]{:S(2)}) async-start(f32[16,1,4096]{2,1,0:T(1,128)} %broadcast_in_dim.36), calls=%async_computation.5 | async-start | bytes 524288 | tf_op jit(solution)/shard_map/all_to_all | solution.py:14
  76.9 0.1 reshape.148
  77.0 0.3 reshape_reshape.3
  77.3 1.1 %copy.21 = f32[32,16,256]{2,0,1:T(8,128)} copy(f32[32,16,256]{2,1,0:T(8,128)S(1)} %reshape_reshape.3) | data formatting | bytes 1048576 | tf_op jit(solution)/shard_map/reshape;reshape | solution.py:25
  78.4 0.0 copy-done
  78.4 6.5 %all-to-all-done.5 = f32[16,1,4096]{2,1,0:T(1,128)S(1)} async-done(((f32[16,1,4096]{2,1,0:T(1,128)}), f32[16,1,4096]{2,1,0:T(1,128)S(1)}, u32[]{:S(2)}, u32[]{:S(2)}) %all-to-all-start.5) | async-done | bytes 262176 | tf_op jit(solution)/shard_map/all_to_all | solution.py:14
  84.9 3.6 %all-to-all-start.1 = ((f32[16,32,256]{2,1,0:T(8,128)}), f32[16,32,256]{2,1,0:T(8,128)S(1)}, u32[]{:S(2)}, u32[]{:S(2)}) async-start(f32[16,32,256]{2,1,0:T(8,128)} %bitcast.13), calls=%async_computation.1 | async-start | bytes 1048576 | tf_op jit(solution)/shard_map/all_to_all | solution.py:30
  88.5 0.6 add_divide_fusion
  89.1 0.2 reduce_sum.101
  89.3 9.3 %all-to-all-done.1 = f32[16,32,256]{2,1,0:T(8,128)S(1)} async-done(((f32[16,32,256]{2,1,0:T(8,128)}), f32[16,32,256]{2,1,0:T(8,128)S(1)}, u32[]{:S(2)}, u32[]{:S(2)}) %all-to-all-start.1) | async-done | bytes 524320 | tf_op jit(solution)/shard_map/all_to_all | solution.py:30
  98.6 0.7 broadcast_in_dim.37
  99.3 3.4 %all-to-all-start.6 = ((f32[8,1,4096]{2,1,0:T(1,128)}), f32[8,1,4096]{2,1,0:T(1,128)S(1)}, u32[]{:S(2)}, u32[]{:S(2)}) async-start(f32[8,1,4096]{2,1,0:T(1,128)} %broadcast_in_dim.37), calls=%async_computation.6 | async-start | bytes 262144 | tf_op jit(solution)/shard_map/all_to_all | solution.py:14
  102.7 0.7 broadcast_divide_fusion
  103.4 5.3 %all-to-all-done.6 = f32[8,1,4096]{2,1,0:T(1,128)S(1)} async-done(((f32[8,1,4096]{2,1,0:T(1,128)}), f32[8,1,4096]{2,1,0:T(1,128)S(1)}, u32[]{:S(2)}, u32[]{:S(2)}) %all-to-all-start.6) | async-done | bytes 131104 | tf_op jit(solution)/shard_map/all_to_all | solution.py:14
  108.7 0.1 reduce_sum.102
  108.8 0.7 div.71
  (9 shorter events, 0.2 us)
Async XLA Ops:
  0.6 13.8 %copy-start.1 = (s32[32]{0:T(128)S(1)}, s32[32]{0:T(128)}, u32[]{:S(2)}) copy-start(s32[32]{0:T(128)} %param.5) | copy-start | bytes 388
  0.6 13.8 %copy-start.2 = (s32[32,1]{0,1:T(1,128)S(1)}, s32[32,1]{0,1:T(1,128)}, u32[]{:S(2)}) copy-start(s32[32,1]{0,1:T(1,128)} %param.4) | copy-start | bytes 388
  6.4 16.0 %all-to-all-start = ((f32[16,1,2048]{2,1,0:T(1,128)}), f32[16,1,2048]{2,1,0:T(1,128)S(1)}, u32[]{:S(2)}, u32[]{:S(2)}) async-start(f32[16,1,2048]{2,1,0:T(1,128)} %reshape.152), calls=%async_computation | async-start | bytes 262144 | tf_op jit(solution)/shard_map/all_to_all | solution.py:14
  24.1 54.3 %copy-start = (f32[32,64]{1,0:T(8,128)}, f32[32,64]{1,0:T(8,128)S(1)}, u32[]{:S(2)}) copy-start(f32[32,64]{1,0:T(8,128)S(1)} %get-tuple-element.12) | copy-start | bytes 24580
  26.1 19.5 %all-to-all-start.3 = ((f32[32,1,65]{2,1,0:T(1,128)}), f32[32,1,65]{2,1,0:T(1,128)S(1)}, u32[]{:S(2)}, u32[]{:S(2)}) async-start(f32[32,1,65]{2,1,0:T(1,128)} %broadcast_in_dim.34), calls=%async_computation.3 | async-start | bytes 32768 | tf_op jit(solution)/shard_map/all_to_all | solution.py:14
  46.2 9.7 %all-to-all-start.4 = ((f32[4,1,65]{2,1,0:T(1,128)}), f32[4,1,65]{2,1,0:T(1,128)S(1)}, u32[]{:S(2)}, u32[]{:S(2)}) async-start(f32[4,1,65]{2,1,0:T(1,128)} %broadcast_in_dim.35), calls=%async_computation.4 | async-start | bytes 4096 | tf_op jit(solution)/shard_map/all_to_all | solution.py:14
  55.9 15.7 %all-to-all-start.2 = ((f32[16,1,4096]{2,1,0:T(1,128)}), f32[16,1,4096]{2,1,0:T(1,128)S(1)}, u32[]{:S(2)}, u32[]{:S(2)}) async-start(f32[16,1,4096]{2,1,0:T(1,128)} %copy.13), calls=%async_computation.2 | async-start | bytes 524288 | tf_op jit(solution)/shard_map/all_to_all | solution.py:30
  72.7 12.2 %all-to-all-start.5 = ((f32[16,1,4096]{2,1,0:T(1,128)}), f32[16,1,4096]{2,1,0:T(1,128)S(1)}, u32[]{:S(2)}, u32[]{:S(2)}) async-start(f32[16,1,4096]{2,1,0:T(1,128)} %broadcast_in_dim.36), calls=%async_computation.5 | async-start | bytes 524288 | tf_op jit(solution)/shard_map/all_to_all | solution.py:14
  84.9 13.7 %all-to-all-start.1 = ((f32[16,32,256]{2,1,0:T(8,128)}), f32[16,32,256]{2,1,0:T(8,128)S(1)}, u32[]{:S(2)}, u32[]{:S(2)}) async-start(f32[16,32,256]{2,1,0:T(8,128)} %bitcast.13), calls=%async_computation.1 | async-start | bytes 1048576 | tf_op jit(solution)/shard_map/all_to_all | solution.py:30
  99.3 9.4 %all-to-all-start.6 = ((f32[8,1,4096]{2,1,0:T(1,128)}), f32[8,1,4096]{2,1,0:T(1,128)S(1)}, u32[]{:S(2)}, u32[]{:S(2)}) async-start(f32[8,1,4096]{2,1,0:T(1,128)} %broadcast_in_dim.37), calls=%async_computation.6 | async-start | bytes 262144 | tf_op jit(solution)/shard_map/all_to_all | solution.py:14
where the time goes:
time: 111 us; the launch traced here: 109 us
  waiting for transfers between devices  38.8 us (35%)
  starting transfers between devices  33.8 us (30%)
  matrix products  15.6 us (14%)
  other arithmetic  11.2 us (10%)
  local copies, waits for them, and re-layouts  7.91 us (7%)
  between operations  2.2 us (2%)
    all_to_all x5, starting transfers between devices, sent_to_all(): lax.all_to_all(jnp.broadcast_to(value[None], (count, *value.shape)), axis...  23.2 us
    all_to_all x5, waiting for transfers between devices, sent_to_all(): lax.all_to_all(jnp.broadcast_to(value[None], (count, *value.shape)), axis...  22.3 us
    all_to_all x2, waiting for transfers between devices, sum_at_owner(): pieces = lax.all_to_all(split_up(value, dim, count), axis, 0, 0, tiled=True)  16.6 us
    dot_general x1, matrix products, local(): jnp.einsum('svc,swc->svw', centered, centered, precision=high)  14.9 us
    all_to_all x2, starting transfers between devices, sum_at_owner(): pieces = lax.all_to_all(split_up(value, dim, count), axis, 0, 0, tiled=True)  10.6 us
    reduce_sum x1, other arithmetic, local(): tile_sum = jnp.sum(jnp.where(live[:, None, :], state, 0.0), axis=2)  4.11 us
    broadcast_in_dim x5, local copies, waits for them, and re-layouts, sent_to_all(): jnp.broadcast_to(value[None], (count, *value.shape))  2.83 us
  transfers between devices with their start and end apart: 7, of which 6 were waited for; matrix products, arithmetic and copies ran while one was open for 20% of the time, Pallas kernels for 0%

commit v1 on v0

v1 whole, which is shorter than its diff:
```python
import jax
import jax.numpy as jnp
from jax import lax
from jax.experimental import pallas as pl
from jax.experimental.pallas import tpu as pltpu
from jax.sharding import PartitionSpec as P

F32 = jnp.float32
HIGH = lax.Precision.HIGHEST
TN = (((0,), (0,)), ((), ()))
NN = (((1,), (0,)), ((), ()))
NT = (((1,), (1,)), ((), ()))

V = 64
ROWS1 = 88
ROWG = 40
ROWS2 = 40


def dot(a, b, dims):
    return lax.dot_general(a, b, dims, precision=HIGH, preferred_element_type=F32)


def iota(shape, dim):
    return lax.broadcasted_iota(jnp.int32, shape, dim)


def slab_of(i):
    return 2 * (i % 16) + i // 16


def spread(get, key):
    out = jnp.zeros(key.shape, F32)
    for i in range(32):
        out = jnp.where(key == i, get(slab_of(i)), out)
    return out


def swap(a):
    return pltpu.roll(a, 64, 1)


def doubled(pairs):
    low = iota(pairs.shape, 1) < V
    other = swap(pairs)
    return jnp.concatenate([jnp.where(low, pairs, other), jnp.where(low, other, pairs)], axis=0)


def halves(a):
    return jnp.where(iota((32, 128), 1) < V, a[:32], a[32:])


def tile_kernel(counts, state, msg, glob, means, sums, stage):
    step = pl.program_id(0)
    first_cell = lax.axis_index("sim") * 1024

    def valid(s):
        return jnp.clip(counts[s] - first_cell, 0, 1024)

    @pl.when(step == 0)
    def _():
        means[...] = jnp.zeros_like(means)
        sums[...] = jnp.zeros_like(sums)

    cell = iota((1, 1024), 1)
    low = iota((64, 128), 1) < V
    for k in range(2):
        pair = 2 * step + k
        parts, mids = [], []
        for q in range(2):
            n = valid(2 * pair + q)
            live = cell < n
            x = state[2 * k + q]
            total = jnp.sum(jnp.where(live, x, 0.0), axis=1, keepdims=True)
            mid = total / jnp.maximum(n, 1).astype(F32)
            parts.append(jnp.where(live, x - mid, 0.0))
            mids.append(mid)
        mid = jnp.concatenate(mids, axis=0)
        means[...] = jnp.where(iota((128, 128), 1) == pair, mid, means[...])
        c = jnp.concatenate(parts, axis=0)
        hi = c.astype(jnp.bfloat16)
        lo = (c - hi.astype(F32)).astype(jnp.bfloat16)
        both = jnp.concatenate([hi, lo], axis=0)
        prod = lax.dot_general(both, both, NT, preferred_element_type=F32)
        left, right = prod[:, :128], prod[:, 128:]
        quad = left[:128] + right[:128] + (left[128:] + right[128:])
        co = jnp.where(low, quad[:64], quad[64:])
        sums[...] += co
        stage[...] = co
        for r in range(4):
            msg[pl.ds(r * 16 + pair, 16, stride=ROWS1), :] = stage[pl.ds(r, 16, stride=4), :]

    @pl.when(step == pl.num_programs(0) - 1)
    def _():
        by_pair = means[...].T[:16]
        for j in range(16):
            msg[ROWS1 * j + 64 : ROWS1 * j + 80, :] = by_pair
        mine = jnp.zeros((16, 128), F32)
        for i in range(8):
            col = means[pl.ds((i // 4) * 64 + i % 4, 16, stride=4), :]
            mine = mine + (pltpu.roll(col, 16 * i, 1) if i else col)
        msg[pl.ds(80, 16, stride=ROWS1), :] = mine
        weight = spread(lambda s: valid(s).astype(F32), iota((32, 128), 0))
        m = doubled(by_pair)
        number = jnp.sum(weight, axis=0, keepdims=True)
        centre = jnp.sum(weight * m, axis=0, keepdims=True) / jnp.maximum(number, 1.0)
        off = m - centre
        between = dot(weight * off, off, TN)[:64]
        acc = sums[...]
        glob[:32, :] = halves(acc + swap(acc) + between)
        glob[32:33, :] = centre
        glob[33:34, :] = number


def slab_kernel(counts, owner, recv, *rest):
    globs = rest[:8]
    slab_mean, slab_cov, msg, stage = rest[8:]
    j = lax.axis_index("sim")

    def count(s):
        return counts[s].astype(F32)

    lane = iota((1, 128), 1)
    acc = recv[0, :64, :]
    for d in range(1, 16):
        acc = acc + recv[d, :64, :]
    lane16 = iota((16, 128), 1)
    sub16 = iota((16, 128), 0)
    cnt_p = spread(count, jnp.where(lane16 < V, sub16, sub16 + 16))
    tile_means = [recv[d, 64:80, :] for d in range(16)]
    total = jnp.zeros((16, 128), F32)
    for d in range(16):
        total = total + jnp.clip(cnt_p - 1024.0 * d, 0.0, 1024.0) * tile_means[d]
    mean_p = total / cnt_p
    cnt_q = spread(count, (lane // 64) * 16 + lane % 16)
    own = jnp.concatenate([recv[d, 80:81, :] for d in range(16)], axis=0)
    w_q = jnp.clip(cnt_q - 1024.0 * sub16.astype(F32), 0.0, 1024.0)
    mean_q = jnp.sum(w_q * own, axis=0, keepdims=True) / cnt_q
    off_q = w_q * (own - mean_q)
    same = lane16 % 16 == sub16
    lhs = jnp.concatenate([jnp.where(same, off_q[d : d + 1], 0.0) for d in range(16)], axis=0)
    rhs = jnp.concatenate([t - mean_p for t in tile_means], axis=0)
    between = dot(lhs, rhs, TN)
    low64 = iota((64, 128), 1) < V
    co = acc + jnp.where(low64, between[:64], between[64:])
    low16 = lane16 < V
    tiles = []
    for t in range(2):
        a, b = co[32 * t : 32 * t + 16], co[32 * t + 16 : 32 * t + 32]
        tiles.append(jnp.concatenate([jnp.where(low16, a, swap(b)), jnp.where(low16, swap(a), b)], axis=0))
    cnt_c = spread(count, iota((32, 128), 0))
    m = doubled(mean_p)
    for par in range(2):
        rows = slice(16 * par, 16 * par + 16)
        stage[0, pl.ds(par, 16, stride=2), :] = m[rows]
        for t in range(2):
            stage[1 + t, pl.ds(par, 16, stride=2), :] = tiles[t][rows] / (cnt_c[rows] - 1.0)
    slab_mean[...] = stage[0, :, :64]
    for t in range(2):
        slab_cov[:, 128 * t : 128 * t + 128] = stage[1 + t]
    names = spread(lambda s: owner[s].astype(F32), iota((1, 128), 1))[:, :32]
    member = (names == iota((16, 32), 0).astype(F32)).astype(F32)
    sizes = dot(member, cnt_c, NN)
    group_mean = dot(member, cnt_c * m, NN) / jnp.maximum(sizes, 1.0)
    off = m - dot(member, group_mean, TN)
    weighted = cnt_c * off
    scale = jnp.maximum(sizes - 1.0, 1.0)
    for t in range(2):
        pick = 4 * j + 2 * t + jnp.where(iota((32, 128), 1) < V, 0, 1)
        inner = tiles[t] + jnp.take_along_axis(weighted, pick, axis=1) * off
        msg[pl.ds(34 + t, 16, stride=ROWS2), :] = dot(member, inner, NN) / scale
    tile_sum = globs[0][:32, :]
    for g in globs[1:]:
        tile_sum = tile_sum + g[:32, :]
    centres = jnp.concatenate([g[32:33, :] for g in globs], axis=0)
    numbers = jnp.concatenate([g[33:34, :] for g in globs], axis=0)
    number = jnp.sum(numbers, axis=0, keepdims=True)
    centre = jnp.sum(numbers * centres, axis=0, keepdims=True) / jnp.maximum(number, 1.0)
    gap = centres - centre
    column = tile_sum + halves(dot(numbers * gap, gap, TN)[:64])
    for d in range(16):
        msg[ROWS2 * d : ROWS2 * d + 32, :] = column
        msg[ROWS2 * d + 32 : ROWS2 * d + 33, :] = centre
        msg[ROWS2 * d + 33 : ROWS2 * d + 34, :] = number


def last_kernel(recv, group_cov, global_mean, global_cov):
    acc = recv[0, :32, :]
    for d in range(1, 16):
        acc = acc + recv[d, :32, :]
    centres = jnp.concatenate([recv[d, 32:33, :] for d in range(16)], axis=0)
    numbers = jnp.concatenate([recv[d, 33:34, :] for d in range(16)], axis=0)
    number = jnp.sum(numbers, axis=0, keepdims=True)
    centre = jnp.sum(numbers * centres, axis=0, keepdims=True) / number
    gap = centres - centre
    spread_all = acc + halves(dot(numbers * gap, gap, TN)[:64])
    out = spread_all / (number - 1.0)
    global_cov[:32, :] = out[:, :64]
    global_cov[32:, :] = swap(out)[:, :64]
    global_mean[...] = centre[:, :64]
    for d in range(16):
        for t in range(2):
            group_cov[:, 256 * d + 128 * t : 256 * d + 128 * t + 128] = recv[d, 34 + t : 35 + t, :]


def local(state, owner, counts):
    smem = pl.BlockSpec(memory_space=pltpu.SMEM)
    vmem = pl.BlockSpec(memory_space=pltpu.VMEM)
    msg, glob = pl.pallas_call(
        tile_kernel,
        grid=(8,),
        in_specs=[smem, pl.BlockSpec((4, V, 1024), lambda i: (i, 0, 0))],
        out_specs=[vmem, vmem],
        out_shape=[
            jax.ShapeDtypeStruct((16 * ROWS1, 128), F32),
            jax.ShapeDtypeStruct((ROWG, 128), F32),
        ],
        scratch_shapes=[
            pltpu.VMEM((128, 128), F32),
            pltpu.VMEM((64, 128), F32),
            pltpu.VMEM((64, 128), F32),
        ],
        name="tile",
    )(counts, state)
    with jax.named_scope("slices"):
        recv = lax.all_to_all(msg.reshape(16, ROWS1, 128), "sim", 0, 0, tiled=True)
    globs = [glob]
    for k in range(1, 8):
        with jax.named_scope(f"sec{k}"):
            globs.append(lax.ppermute(glob, "section", [(i, (i + k) % 8) for i in range(8)]))
    slab_mean, slab_cov, msg2 = pl.pallas_call(
        slab_kernel,
        in_specs=[smem, smem] + [vmem] * 9,
        out_specs=[vmem] * 3,
        out_shape=[
            jax.ShapeDtypeStruct((32, 64), F32),
            jax.ShapeDtypeStruct((32, 256), F32),
            jax.ShapeDtypeStruct((16 * ROWS2, 128), F32),
        ],
        scratch_shapes=[pltpu.VMEM((3, 32, 128), F32)],
        name="slab",
    )(counts, owner[:, 0], recv, *globs)
    with jax.named_scope("groups"):
        recv2 = lax.all_to_all(msg2.reshape(16, ROWS2, 128), "sim", 0, 0, tiled=True)
    group_cov, global_mean, global_cov = pl.pallas_call(
        last_kernel,
        in_specs=[vmem],
        out_specs=[vmem] * 3,
        out_shape=[
            jax.ShapeDtypeStruct((1, 4096), F32),
            jax.ShapeDtypeStruct((1, 64), F32),
            jax.ShapeDtypeStruct((64, 64), F32),
        ],
        name="last",
    )(recv2)
    return slab_mean, slab_cov, group_cov, global_mean.reshape(64), global_cov


def solution(mesh):
    return jax.shard_map(
        local,
        mesh=mesh,
        in_specs=(P("section", None, "sim"), P("section", None), P("section")),
        out_specs=(P("section", None), P("section", "sim"), P(("section", "sim"), None), P(), P()),
        check_vma=False,
    )
```

time: 111 us -> 53.4 us (0.48)
  waiting for transfers between devices: 38.8 us -> 5.88 us
  starting transfers between devices: 33.8 us -> 15.8 us
  matrix products: 15.6 us -> 0 us
  blocking collectives: 0 us -> 14.9 us
  Pallas kernels: 0 us -> 14.8 us
  other arithmetic: 11.2 us -> 0 us
  local copies, waits for them, and re-layouts: 7.91 us -> 0.86 us
  between operations: 2.2 us -> 0.69 us
    all_to_all x7 -> x1, waiting for transfers between devices: 38.8 us -> 1.75 us  [local(): recv = lax.all_to_all(msg.reshape(16, ROWS1, 128), 'sim', 0, 0, tiled=True)]
    all_to_all x7 -> x1, starting transfers between devices: 33.8 us -> 7.99 us  [local(): recv = lax.all_to_all(msg.reshape(16, ROWS1, 128), 'sim', 0, 0, tiled=True)]
    dot_general x3 -> x0, matrix products: 15.6 us -> none  [the longest x1 14.9 us: local(): jnp.einsum('svc,swc->svw', centered, centered, precision=high)]
    all_to_all x0 -> x1, blocking collectives: none -> 14.9 us  [local(): lax.all_to_all(msg2.reshape(16, ROWS2, 128), 'sim', 0, 0, tiled=True)]
    pallas_call x0 -> x3, Pallas kernels: none -> 14.8 us  [the longest x1 9.95 us: local(): pl.pallas_call(tile_kernel, grid=(8,), in_specs=[smem, pl.BlockSpec((4, V...]
    ppermute x0 -> x7, starting transfers between devices: none -> 7.83 us  [local(): lax.ppermute(glob, 'section', [(i, (i + k) % 8) for i in range(8)])]
    reduce_sum x10 -> x0, other arithmetic: 5.37 us -> none  [the longest x1 4.11 us: local(): tile_sum = jnp.sum(jnp.where(live[:, None, :], state, 0.0), axis=2)]
    ppermute x0 -> x7, waiting for transfers between devices: none -> 4.13 us  [local(): lax.ppermute(glob, 'section', [(i, (i + k) % 8) for i in range(8)])]
  transfers between devices with their start and end apart: 7 -> 8, of which waited for: 6 -> 5; matrix products, arithmetic and copies ran while one was open for 20% -> 0% of each run, Pallas kernels for 0% -> 0%
where the time goes in v1:
time: 53.4 us; the launch traced here: 52.9 us
  starting transfers between devices  15.8 us (30%)
  blocking collectives  14.9 us (28%)
  Pallas kernels  14.8 us (28%)
  waiting for transfers between devices  5.88 us (11%)
  local copies, waits for them, and re-layouts  0.86 us (2%)
  between operations  0.69 us (1%)
    all_to_all x1, blocking collectives, local(): lax.all_to_all(msg2.reshape(16, ROWS2, 128), 'sim', 0, 0, tiled=True)  14.9 us
    pallas_call x1, Pallas kernels, local(): pl.pallas_call(tile_kernel, grid=(8,), in_specs=[smem, pl.BlockSpec((4, V...  9.95 us
    all_to_all x1, starting transfers between devices, local(): recv = lax.all_to_all(msg.reshape(16, ROWS1, 128), 'sim', 0, 0, tiled=True)  7.99 us
    ppermute x7, starting transfers between devices, local(): lax.ppermute(glob, 'section', [(i, (i + k) % 8) for i in range(8)])  7.83 us
    ppermute x7, waiting for transfers between devices, local(): lax.ppermute(glob, 'section', [(i, (i + k) % 8) for i in range(8)])  4.13 us
    pallas_call x1, Pallas kernels, local(): pl.pallas_call(slab_kernel, in_specs=[smem, smem] + [vmem] * 9, out_specs...  2.88 us
    pallas_call x1, Pallas kernels, local(): pl.pallas_call(last_kernel, in_specs=[vmem], out_specs=[vmem] * 3, out_sh...  1.94 us
    all_to_all x1, waiting for transfers between devices, local(): recv = lax.all_to_all(msg.reshape(16, ROWS1, 128), 'sim', 0, 0, tiled=True)  1.75 us
  transfers between devices with their start and end apart: 8, of which 5 were waited for; matrix products, arithmetic and copies ran while one was open for 0% of the time, Pallas kernels for 0%

profile of v1, /device:TPU:0, one launch (start us, length us, event | category | flops | bytes accessed | tf_op | source)
XLA Modules:
  0.0 52.9 jit_solution(13135267238664599934)
XLA Ops:
  0.6 10.0 %tile.1 = (f32[1408,128]{1,0:T(8,128)}, f32[40,128]{1,0:T(8,128)}) custom-call(s32[32]{0:T(128)} %counts.3, f32[32,64,1024]{2,1,0:T(8,128)} %state.1), custom_call_target="tpu_custom_call" | custom-call | tf_op jit(solution)/shard_map/tile/pallas_call | solution.py:209
  10.6 8.0 %all-to-all-start = ((f32[16,88,128]{2,1,0:T(8,128)}), f32[16,88,128]{2,1,0:T(8,128)S(1)}, u32[]{:S(2)}, u32[]{:S(2)}) async-start(f32[16,88,128]{2,1,0:T(8,128)} %bitcast.4), calls=%async_computation | async-start | bytes 1441792 | tf_op jit(solution)/shard_map/slices/all_to_all | solution.py:226
  18.6 2.2 %collective-permute-start.6 = (f32[40,128]{1,0:T(8,128)}, f32[40,128]{1,0:T(8,128)S(1)}, u32[]{:S(2)}, u32[]{:S(2)}) collective-permute-start(f32[40,128]{1,0:T(8,128)} %get-tuple-element.14.rest_0_), channel_id=1, source_target_pairs={{0,112},{16,0},{32,16},{48,32},{64,48},{80,64},{96,80},{112,96},{1... | collective-permute-start | bytes 61448 | tf_op jit(solution)/shard_map/sec7/ppermute | solution.py:230
  20.8 0.9 %collective-permute-start.5 = (f32[40,128]{1,0:T(8,128)}, f32[40,128]{1,0:T(8,128)S(1)}, u32[]{:S(2)}, u32[]{:S(2)}) collective-permute-start(f32[40,128]{1,0:T(8,128)} %get-tuple-element.14.rest_0_), channel_id=1, source_target_pairs={{0,96},{16,112},{32,0},{48,16},{64,32},{80,48},{96,64},{112,80},{1... | collective-permute-start | bytes 61448 | tf_op jit(solution)/shard_map/sec6/ppermute | solution.py:230
  21.7 0.4 collective-permute-start.4
  22.1 2.9 %collective-permute-start.3 = (f32[40,128]{1,0:T(8,128)}, f32[40,128]{1,0:T(8,128)S(1)}, u32[]{:S(2)}, u32[]{:S(2)}) collective-permute-start(f32[40,128]{1,0:T(8,128)} %get-tuple-element.14.rest_0_), channel_id=1, source_target_pairs={{0,64},{16,80},{32,96},{48,112},{64,0},{80,16},{96,32},{112,48},{1... | collective-permute-start | bytes 61448 | tf_op jit(solution)/shard_map/sec4/ppermute | solution.py:230
  25.0 0.0 collective-permute-start.2
  25.0 0.0 collective-permute-done.6.rest_7_
  25.0 0.0 copy-start.1
  25.0 0.4 collective-permute-start.1
  25.4 0.0 collective-permute-done.5.rest_6_
  25.4 0.0 copy-start.2
  25.4 1.0 %collective-permute-start = (f32[40,128]{1,0:T(8,128)}, f32[40,128]{1,0:T(8,128)S(1)}, u32[]{:S(2)}, u32[]{:S(2)}) collective-permute-start(f32[40,128]{1,0:T(8,128)} %get-tuple-element.14.rest_0_), channel_id=1, source_target_pairs={{0,16},{16,32},{32,48},{48,64},{64,80},{80,96},{96,112},{112,0},{1... | collective-permute-start | bytes 61448 | tf_op jit(solution)/shard_map/sec1/ppermute | solution.py:230
  26.4 0.0 collective-permute-done.4.rest_5_
  26.4 0.0 copy-start.3
  26.4 1.1 %collective-permute-done.3.rest_4_ = f32[40,128]{1,0:T(8,128)S(1)} collective-permute-done((f32[40,128]{1,0:T(8,128)}, f32[40,128]{1,0:T(8,128)S(1)}, u32[]{:S(2)}, u32[]{:S(2)}) %collective-permute-start.3) | collective-permute-done | bytes 20512 | tf_op jit(solution)/shard_map/sec4/ppermute | solution.py:230
  27.6 0.0 copy-start.4
  27.6 2.3 %collective-permute-done.2.rest_3_ = f32[40,128]{1,0:T(8,128)S(1)} collective-permute-done((f32[40,128]{1,0:T(8,128)}, f32[40,128]{1,0:T(8,128)S(1)}, u32[]{:S(2)}, u32[]{:S(2)}) %collective-permute-start.2) | collective-permute-done | bytes 20512 | tf_op jit(solution)/shard_map/sec3/ppermute | solution.py:230
  29.9 0.0 copy-start.5
  29.9 0.6 %collective-permute-done.1.rest_2_ = f32[40,128]{1,0:T(8,128)S(1)} collective-permute-done((f32[40,128]{1,0:T(8,128)}, f32[40,128]{1,0:T(8,128)S(1)}, u32[]{:S(2)}, u32[]{:S(2)}) %collective-permute-start.1) | collective-permute-done | bytes 20512 | tf_op jit(solution)/shard_map/sec2/ppermute | solution.py:230
  30.5 0.0 copy-start.6
  30.5 0.1 collective-permute-done.rest_1_
  30.6 0.0 copy-start.7
  30.6 1.7 %all-to-all-done.recv = f32[16,88,128]{2,1,0:T(8,128)S(1)} async-done(((f32[16,88,128]{2,1,0:T(8,128)}), f32[16,88,128]{2,1,0:T(8,128)S(1)}, u32[]{:S(2)}, u32[]{:S(2)}) %all-to-all-start) | async-done | bytes 720928 | tf_op jit(solution)/shard_map/slices/all_to_all | solution.py:226
  32.3 0.0 copy-start
  32.3 0.0 copy-done.1
  32.3 0.0 copy-done.2
  32.3 0.0 copy-done.3
  32.3 0.0 copy-done.4
  32.3 0.0 copy-done.5
  32.3 0.0 copy-done.6
  32.3 0.0 copy-done.7
  32.4 0.8 %copy-done = f32[16,88,128]{2,1,0:T(8,128)} copy-done((f32[16,88,128]{2,1,0:T(8,128)}, f32[16,88,128]{2,1,0:T(8,128)S(1)}, u32[]{:S(2)}) %copy-start) | copy-done | bytes 720920
  33.2 2.9 %slab.1 = (f32[32,64]{1,0:T(8,128)}, f32[32,256]{1,0:T(8,128)}, f32[640,128]{1,0:T(8,128)}) custom-call(s32[32]{0:T(128)} %counts.3, s32[32]{0:T(128)} %bitcast.6, f32[16,88,128]{2,1,0:T(8,128)} %copy-done, f32[40,128]{1,0:T(8,128)} %get-tuple-element.14.rest_0_, f32[40,128]{1,0:T(8,128)} %copy-done.7, f32[40,128]{1,0:T(8,128)} %copy-done.6, ...), custom_call_target="tpu_custom_call" | custom-call | tf_op jit(solution)/shard_map/slab/pallas_call | solution.py:231
  36.1 14.9 %all_to_all.10.recv = f32[16,40,128]{2,1,0:T(8,128)} all-to-all(f32[16,40,128]{2,1,0:T(8,128)} %bitcast.5), channel_id=1, replica_groups=mesh['section'=8,'sim'=16] {'sim'}, dimensions={0} | all-to-all | bytes 655360 | tf_op jit(solution)/shard_map/groups/all_to_all | solution.py:244
  51.0 1.9 %last.1 = (f32[1,4096]{1,0:T(1,128)}, f32[1,64]{1,0:T(1,128)}, f32[64,64]{1,0:T(8,128)}) custom-call(f32[16,40,128]{2,1,0:T(8,128)} %all_to_all.10.recv), custom_call_target="tpu_custom_call" | custom-call | tf_op jit(solution)/shard_map/last/pallas_call | solution.py:245
Async XLA Ops:
  10.6 21.7 %all-to-all-start = ((f32[16,88,128]{2,1,0:T(8,128)}), f32[16,88,128]{2,1,0:T(8,128)S(1)}, u32[]{:S(2)}, u32[]{:S(2)}) async-start(f32[16,88,128]{2,1,0:T(8,128)} %bitcast.4), calls=%async_computation | async-start | bytes 1441792 | tf_op jit(solution)/shard_map/slices/all_to_all | solution.py:226
  18.6 6.4 %collective-permute-start.6 = (f32[40,128]{1,0:T(8,128)}, f32[40,128]{1,0:T(8,128)S(1)}, u32[]{:S(2)}, u32[]{:S(2)}) collective-permute-start(f32[40,128]{1,0:T(8,128)} %get-tuple-element.14.rest_0_), channel_id=1, source_target_pairs={{0,112},{16,0},{32,16},{48,32},{64,48},{80,64},{96,80},{112,96},{1... | collective-permute-start | bytes 61448 | tf_op jit(solution)/shard_map/sec7/ppermute | solution.py:230
  20.8 4.6 %collective-permute-start.5 = (f32[40,128]{1,0:T(8,128)}, f32[40,128]{1,0:T(8,128)S(1)}, u32[]{:S(2)}, u32[]{:S(2)}) collective-permute-start(f32[40,128]{1,0:T(8,128)} %get-tuple-element.14.rest_0_), channel_id=1, source_target_pairs={{0,96},{16,112},{32,0},{48,16},{64,32},{80,48},{96,64},{112,80},{1... | collective-permute-start | bytes 61448 | tf_op jit(solution)/shard_map/sec6/ppermute | solution.py:230
  21.7 4.7 %collective-permute-start.4 = (f32[40,128]{1,0:T(8,128)}, f32[40,128]{1,0:T(8,128)S(1)}, u32[]{:S(2)}, u32[]{:S(2)}) collective-permute-start(f32[40,128]{1,0:T(8,128)} %get-tuple-element.14.rest_0_), channel_id=1, source_target_pairs={{0,80},{16,96},{32,112},{48,0},{64,16},{80,32},{96,48},{112,64},{1... | collective-permute-start | bytes 61448 | tf_op jit(solution)/shard_map/sec5/ppermute | solution.py:230
  22.1 5.5 %collective-permute-start.3 = (f32[40,128]{1,0:T(8,128)}, f32[40,128]{1,0:T(8,128)S(1)}, u32[]{:S(2)}, u32[]{:S(2)}) collective-permute-start(f32[40,128]{1,0:T(8,128)} %get-tuple-element.14.rest_0_), channel_id=1, source_target_pairs={{0,64},{16,80},{32,96},{48,112},{64,0},{80,16},{96,32},{112,48},{1... | collective-permute-start | bytes 61448 | tf_op jit(solution)/shard_map/sec4/ppermute | solution.py:230
  25.0 4.9 %collective-permute-start.2 = (f32[40,128]{1,0:T(8,128)}, f32[40,128]{1,0:T(8,128)S(1)}, u32[]{:S(2)}, u32[]{:S(2)}) collective-permute-start(f32[40,128]{1,0:T(8,128)} %get-tuple-element.14.rest_0_), channel_id=1, source_target_pairs={{0,48},{16,64},{32,80},{48,96},{64,112},{80,0},{96,16},{112,32},{1... | collective-permute-start | bytes 61448 | tf_op jit(solution)/shard_map/sec3/ppermute | solution.py:230
  25.0 7.3 %copy-start.1 = (f32[40,128]{1,0:T(8,128)}, f32[40,128]{1,0:T(8,128)S(1)}, u32[]{:S(2)}) copy-start(f32[40,128]{1,0:T(8,128)S(1)} %collective-permute-done.6.rest_7_) | copy-start | bytes 61444
  25.0 5.5 %collective-permute-start.1 = (f32[40,128]{1,0:T(8,128)}, f32[40,128]{1,0:T(8,128)S(1)}, u32[]{:S(2)}, u32[]{:S(2)}) collective-permute-start(f32[40,128]{1,0:T(8,128)} %get-tuple-element.14.rest_0_), channel_id=1, source_target_pairs={{0,32},{16,48},{32,64},{48,80},{64,96},{80,112},{96,0},{112,16},{1... | collective-permute-start | bytes 61448 | tf_op jit(solution)/shard_map/sec2/ppermute | solution.py:230
  25.4 6.9 %copy-start.2 = (f32[40,128]{1,0:T(8,128)}, f32[40,128]{1,0:T(8,128)S(1)}, u32[]{:S(2)}) copy-start(f32[40,128]{1,0:T(8,128)S(1)} %collective-permute-done.5.rest_6_) | copy-start | bytes 61444
  25.4 5.2 %collective-permute-start = (f32[40,128]{1,0:T(8,128)}, f32[40,128]{1,0:T(8,128)S(1)}, u32[]{:S(2)}, u32[]{:S(2)}) collective-permute-start(f32[40,128]{1,0:T(8,128)} %get-tuple-element.14.rest_0_), channel_id=1, source_target_pairs={{0,16},{16,32},{32,48},{48,64},{64,80},{80,96},{96,112},{112,0},{1... | collective-permute-start | bytes 61448 | tf_op jit(solution)/shard_map/sec1/ppermute | solution.py:230
  26.4 5.9 %copy-start.3 = (f32[40,128]{1,0:T(8,128)}, f32[40,128]{1,0:T(8,128)S(1)}, u32[]{:S(2)}) copy-start(f32[40,128]{1,0:T(8,128)S(1)} %collective-permute-done.4.rest_5_) | copy-start | bytes 61444
  27.6 4.8 %copy-start.4 = (f32[40,128]{1,0:T(8,128)}, f32[40,128]{1,0:T(8,128)S(1)}, u32[]{:S(2)}) copy-start(f32[40,128]{1,0:T(8,128)S(1)} %collective-permute-done.3.rest_4_) | copy-start | bytes 61444
  29.9 2.4 %copy-start.5 = (f32[40,128]{1,0:T(8,128)}, f32[40,128]{1,0:T(8,128)S(1)}, u32[]{:S(2)}) copy-start(f32[40,128]{1,0:T(8,128)S(1)} %collective-permute-done.2.rest_3_) | copy-start | bytes 61444
  30.5 1.9 %copy-start.6 = (f32[40,128]{1,0:T(8,128)}, f32[40,128]{1,0:T(8,128)S(1)}, u32[]{:S(2)}) copy-start(f32[40,128]{1,0:T(8,128)S(1)} %collective-permute-done.1.rest_2_) | copy-start | bytes 61444
  30.6 1.8 %copy-start.7 = (f32[40,128]{1,0:T(8,128)}, f32[40,128]{1,0:T(8,128)S(1)}, u32[]{:S(2)}) copy-start(f32[40,128]{1,0:T(8,128)S(1)} %collective-permute-done.rest_1_) | copy-start | bytes 61444
  32.3 0.9 %copy-start = (f32[16,88,128]{2,1,0:T(8,128)}, f32[16,88,128]{2,1,0:T(8,128)S(1)}, u32[]{:S(2)}) copy-start(f32[16,88,128]{2,1,0:T(8,128)S(1)} %all-to-all-done.recv) | copy-start | bytes 2162692

commit v2 on v1

v2 whole, which is shorter than its diff:
```python
import functools

import jax
import jax.numpy as jnp
from jax import lax
from jax.experimental import pallas as pl
from jax.experimental.pallas import tpu as pltpu
from jax.sharding import PartitionSpec as P

F32 = jnp.float32
HIGH = lax.Precision.HIGHEST
NN = (((1,), (0,)), ((), ()))
TN = (((0,), (0,)), ((), ()))
NT = (((1,), (1,)), ((), ()))

V = 64
CHUNK = 4
MIB = 1 << 20
ROWS1 = 80
MEANS = 64
ROWS = 24
DIAG = 16
CENTRE = 17
NUMBER = 18
GROUP = 19


def dot(a, b, dims):
    return lax.dot_general(a, b, dims, precision=HIGH, preferred_element_type=F32)


def iota(shape, dim):
    return lax.broadcasted_iota(jnp.int32, shape, dim)


def slab_of(i):
    return 2 * (i % 16) + i // 16


def spread(get, key):
    out = jnp.zeros(key.shape, F32)
    for i in range(32):
        out = jnp.where(key == i, get(slab_of(i)), out)
    return out


def swap(a):
    return pltpu.roll(a, 64, 1)


def doubled(pairs):
    low = iota(pairs.shape, 1) < V
    other = swap(pairs)
    return jnp.concatenate([jnp.where(low, pairs, other), jnp.where(low, other, pairs)], axis=0)


def packed(a):
    v, w = iota((32, 128), 0), iota((32, 128), 1) % V
    last = pltpu.roll(a[32:], 32, 1)
    body = jnp.where(w < v, last, a[:32])
    diag = jnp.sum(jnp.where(w == v, last, 0.0), axis=0, keepdims=True)
    return jnp.where(iota((16, 128), 1) < V, body[:16], body[16:]), diag


def unpacked(rows, diag):
    v, w = iota((32, 128), 0), iota((32, 128), 1) % V
    other, low = swap(rows), iota((16, 128), 1) < V
    body = jnp.concatenate([jnp.where(low, rows, other), jnp.where(low, other, rows)], axis=0)
    last, diag = pltpu.roll(body, 32, 1), pltpu.roll(diag, 32, 1)
    upper = jnp.where(w > v, body, jnp.where(w == v, 0.5 * body, 0.0))
    lower = jnp.where(w == v + 32, 0.5 * diag, jnp.where((w >= 32) & (w < v + 32), last, 0.0))
    half = jnp.concatenate([upper, lower], axis=0)
    return half + jnp.concatenate([half, half], axis=0).T[:64]


def put(ref, base, rows, diag, centre, number):
    ref[base : base + 16, :] = rows
    ref[base + DIAG : base + DIAG + 1, :] = diag
    ref[base + CENTRE : base + CENTRE + 1, :] = centre
    ref[base + NUMBER : base + NUMBER + 1, :] = number


def merged(parts):
    rows, diag = parts[0][:16, :], parts[0][DIAG : DIAG + 1, :]
    for p in parts[1:]:
        rows, diag = rows + p[:16, :], diag + p[DIAG : DIAG + 1, :]
    centres = jnp.concatenate([p[CENTRE : CENTRE + 1, :] for p in parts], axis=0)
    numbers = jnp.concatenate([p[NUMBER : NUMBER + 1, :] for p in parts], axis=0)
    number = jnp.sum(numbers, axis=0, keepdims=True)
    centre = jnp.sum(numbers * centres, axis=0, keepdims=True) / jnp.maximum(number, 1.0)
    gap = centres - centre
    more_rows, more_diag = packed(dot(numbers * gap, gap, TN)[:V])
    return rows + more_rows, diag + more_diag, centre, number


def merge_kernel(*refs):
    put(refs[-1], 0, *merged(refs[:-1]))


def copy_in(state, held, sems, i):
    rows = pl.ds(CHUNK * i, CHUNK)
    return pltpu.make_async_copy(state.at[rows], held.at[rows], sems.at[i])


def tile_kernel(counts_in, state, msg, glob, counts, held, mids, means, sums, stage, sem, sems):
    first_cell = lax.axis_index("sim") * 1024
    chunks = 32 // CHUNK
    for i in range(chunks):
        copy_in(state, held, sems, i).start()
        if i == 0:
            counted = pltpu.make_async_copy(counts_in, counts, sem)
            counted.start()
    means[...] = jnp.zeros_like(means)
    sums[...] = jnp.zeros_like(sums)

    def valid(s):
        return jnp.clip(counts[s] - first_cell, 0, 1024)

    cell = iota((1, 1024), 1)
    low = iota((64, 128), 1) < V

    def average(i):
        for k in range(CHUNK):
            s = CHUNK * i + k
            n = valid(s)
            total = jnp.sum(jnp.where(cell < n, held[s], 0.0), axis=1, keepdims=True)
            mids[s] = jnp.broadcast_to(total / jnp.maximum(n, 1).astype(F32), (V, 128))

    def multiply(i):
        for k in range(CHUNK // 2):
            pair = CHUNK // 2 * i + k
            parts = []
            for q in range(2):
                s = 2 * pair + q
                mid = mids[s]
                mean_rows = pl.ds(V * q, V)
                means[mean_rows, :] = jnp.where(iota((V, 128), 1) == pair, mid, means[mean_rows, :])
                x = held[s]
                off = jnp.concatenate([x[:, 128 * t : 128 * t + 128] - mid for t in range(8)], axis=1)
                parts.append(jnp.where(cell < valid(s), off, 0.0))
            c = jnp.concatenate(parts, axis=0)
            hi = c.astype(jnp.bfloat16)
            lo = (c - hi.astype(F32)).astype(jnp.bfloat16)
            both = jnp.concatenate([hi, lo], axis=0)
            prod = lax.dot_general(both, both, NT, preferred_element_type=F32)
            left, right = prod[:, :128], prod[:, 128:]
            quad = left[:128] + right[:128] + (left[128:] + right[128:])
            co = jnp.where(low, quad[:64], quad[64:])
            sums[...] += co
            stage[k] = co
            for r in range(4):
                msg[pl.ds(r * 16 + pair, 16, stride=ROWS1), :] = stage[k, pl.ds(r, 16, stride=4), :]

    counted.wait()
    copy_in(state, held, sems, 0).wait()
    average(0)

    @pl.loop(0, chunks - 1)
    def _(i):
        copy_in(state, held, sems, i + 1).wait()
        average(i + 1)
        multiply(i)

    multiply(chunks - 1)
    by_pair = means[...].T[:16]
    for j in range(16):
        msg[ROWS1 * j + MEANS : ROWS1 * j + MEANS + 16, :] = by_pair
    weight = spread(lambda s: valid(s).astype(F32), iota((32, 128), 0))
    m = doubled(by_pair)
    number = jnp.sum(weight, axis=0, keepdims=True)
    centre = jnp.sum(weight * m, axis=0, keepdims=True) / jnp.maximum(number, 1.0)
    off = m - centre
    acc = sums[...]
    put(glob, 0, *packed(acc + swap(acc) + dot(weight * off, off, TN)[:V]), centre, number)


def slab_kernel(counts, owner, recv, *rest):
    globs = rest[:2]
    slab_mean, slab_cov, msg, stage = rest[2:]
    j = lax.axis_index("sim")

    def count(s):
        return counts[s].astype(F32)

    acc = recv[0, :64, :]
    for d in range(1, 16):
        acc = acc + recv[d, :64, :]
    lane16 = iota((16, 128), 1)
    sub16 = iota((16, 128), 0)
    cnt_p = spread(count, jnp.where(lane16 < V, sub16, sub16 + 16))
    points = jnp.concatenate([recv[d, MEANS : MEANS + 16, :] for d in range(16)], axis=0)
    weight = jnp.concatenate([jnp.clip(cnt_p - 1024.0 * d, 0.0, 1024.0) for d in range(16)], axis=0)

    def over_tiles(a):
        return sum(a[16 * d : 16 * d + 16] for d in range(16))

    mean_p = over_tiles(weight * points) / cnt_p
    off = points - jnp.concatenate([mean_p] * 16, axis=0)
    weighted = weight * off
    co = []
    for r in range(4):
        pick = 4 * j + r + jnp.where(iota((256, 128), 1) < V, 0, V)
        between = over_tiles(jnp.take_along_axis(weighted, pick, axis=1) * off)
        co.append(acc[16 * r : 16 * r + 16] + between)
    low16 = lane16 < V
    tiles = []
    for t in range(2):
        a, b = co[2 * t], co[2 * t + 1]
        tiles.append(jnp.concatenate([jnp.where(low16, a, swap(b)), jnp.where(low16, swap(a), b)], axis=0))
    cnt_c = spread(count, iota((32, 128), 0))
    m = doubled(mean_p)
    for par in range(2):
        rows = slice(16 * par, 16 * par + 16)
        stage[0, pl.ds(par, 16, stride=2), :] = m[rows]
        for t in range(2):
            stage[1 + t, pl.ds(par, 16, stride=2), :] = tiles[t][rows] / (cnt_c[rows] - 1.0)
    slab_mean[...] = stage[0, :, :64]
    for t in range(2):
        slab_cov[:, 128 * t : 128 * t + 128] = stage[1 + t]
    names = spread(lambda s: owner[s].astype(F32), iota((1, 128), 1))[:, :32]
    member = (names == iota((16, 32), 0).astype(F32)).astype(F32)
    sizes = dot(member, cnt_c, NN)
    group_mean = dot(member, cnt_c * m, NN) / jnp.maximum(sizes, 1.0)
    off = m - dot(member, group_mean, TN)
    weighted = cnt_c * off
    scale = jnp.maximum(sizes - 1.0, 1.0)
    for t in range(2):
        pick = 4 * j + 2 * t + jnp.where(iota((32, 128), 1) < V, 0, 1)
        inner = tiles[t] + jnp.take_along_axis(weighted, pick, axis=1) * off
        msg[pl.ds(GROUP + t, 16, stride=ROWS), :] = dot(member, inner, NN) / scale
    column = merged(globs)
    for d in range(16):
        put(msg, ROWS * d, *column)


def last_kernel(recv, group_cov, global_mean, global_cov):
    rows, diag, centre, number = merged([recv.at[d] for d in range(16)])
    global_cov[...] = (unpacked(rows, diag) / (number - 1.0))[:, :V]
    global_mean[...] = centre[:, :V]
    for d in range(16):
        for t in range(2):
            k = 2 * d + t
            group_cov[:, 128 * k : 128 * k + 128] = recv[d, GROUP + t : GROUP + t + 1, :]


def local(state, owner, counts):
    smem = pl.BlockSpec(memory_space=pltpu.SMEM)
    vmem = pl.BlockSpec(memory_space=pltpu.VMEM)
    hbm = functools.partial(pltpu.with_memory_space_constraint, memory_space=pltpu.HBM)
    state, counts, owner = hbm(state), hbm(counts), hbm(owner[:, 0])
    msg, glob = pl.pallas_call(
        tile_kernel,
        in_specs=[pl.BlockSpec(memory_space=pl.ANY)] * 2,
        out_specs=[vmem, vmem],
        out_shape=[
            jax.ShapeDtypeStruct((16 * ROWS1, 128), F32),
            jax.ShapeDtypeStruct((ROWS, 128), F32),
        ],
        scratch_shapes=[
            pltpu.SMEM((32,), jnp.int32),
            pltpu.VMEM((32, V, 1024), F32),
            pltpu.VMEM((32, V, 128), F32),
            pltpu.VMEM((128, 128), F32),
            pltpu.VMEM((64, 128), F32),
            pltpu.VMEM((CHUNK // 2, 64, 128), F32),
            pltpu.SemaphoreType.DMA,
            pltpu.SemaphoreType.DMA((32 // CHUNK,)),
        ],
        compiler_params=pltpu.CompilerParams(vmem_limit_bytes=20 * MIB),
        name="tile",
    )(counts, state)
    with jax.named_scope("slices"):
        recv = lax.all_to_all(msg.reshape(16, ROWS1, 128), "sim", 0, 0, tiled=True)
    parts = [glob]
    for k in range(1, 4):
        with jax.named_scope(f"along_y{k}"):
            pairs = [(i, (i + 2 * k) % 8) for i in range(8)]
            parts.append(lax.ppermute(glob, "section", pairs))
    four = pl.pallas_call(
        merge_kernel,
        in_specs=[vmem] * 4,
        out_specs=vmem,
        out_shape=jax.ShapeDtypeStruct((ROWS, 128), F32),
        compiler_params=pltpu.CompilerParams(vmem_limit_bytes=2 * MIB),
        name="merge",
    )(*parts)
    with jax.named_scope("cores"):
        other = lax.ppermute(four, "section", [(i, i ^ 1) for i in range(8)])
    slab_mean, slab_cov, msg2 = pl.pallas_call(
        slab_kernel,
        in_specs=[smem, smem] + [vmem] * 3,
        out_specs=[vmem] * 3,
        out_shape=[
            jax.ShapeDtypeStruct((32, 64), F32),
            jax.ShapeDtypeStruct((32, 256), F32),
            jax.ShapeDtypeStruct((16 * ROWS, 128), F32),
        ],
        scratch_shapes=[pltpu.VMEM((3, 32, 128), F32)],
        compiler_params=pltpu.CompilerParams(vmem_limit_bytes=4 * MIB),
        name="slab",
    )(counts, owner, recv, four, other)
    with jax.named_scope("groups"):
        recv2 = lax.all_to_all(msg2.reshape(16, ROWS, 128), "sim", 0, 0, tiled=True)
    group_cov, global_mean, global_cov = pl.pallas_call(
        last_kernel,
        in_specs=[vmem],
        out_specs=[vmem] * 3,
        out_shape=[
            jax.ShapeDtypeStruct((1, 4096), F32),
            jax.ShapeDtypeStruct((1, 64), F32),
            jax.ShapeDtypeStruct((64, 64), F32),
        ],
        compiler_params=pltpu.CompilerParams(vmem_limit_bytes=2 * MIB),
        name="last",
    )(recv2)
    return slab_mean, slab_cov, group_cov, global_mean.reshape(64), global_cov


def solution(mesh):
    return jax.shard_map(
        local,
        mesh=mesh,
        in_specs=(P("section", None, "sim"), P("section", None), P("section")),
        out_specs=(P("section", None), P("section", "sim"), P(("section", "sim"), None), P(), P()),
        check_vma=False,
    )
```

time: 53.4 us -> 44.2 us (0.83)
  Pallas kernels: 14.8 us -> 10.1 us
  starting transfers between devices: 15.8 us -> 12.8 us
  blocking collectives: 14.9 us -> 12.6 us
  waiting for transfers between devices: 5.88 us -> 7.81 us
  local copies, waits for them, and re-layouts: 0.86 us -> 0 us
    pallas_call x2 -> x3, Pallas kernels: 12.8 us -> 8.92 us  [the longest x1 6.74 us: local(): pl.pallas_call(tile_kernel, in_specs=[pl.BlockSpec(memory_space=pl.ANY)]...]
    ppermute x7 -> x4, starting transfers between devices: 7.83 us -> 4.77 us  [the longest x3 4.68 us: local(): parts.append(lax.ppermute(glob, 'section', pairs))]
    all_to_all x1, blocking collectives: 14.9 us -> 12.6 us  [local(): recv2 = lax.all_to_all(msg2.reshape(16, ROWS, 128), 'sim', 0, 0, tiled=True)]
    ppermute x7 -> x4, waiting for transfers between devices: 4.13 us -> 5.1 us  [the longest x3 3.93 us: local(): parts.append(lax.ppermute(glob, 'section', pairs))]
    all_to_all x1, waiting for transfers between devices: 1.75 us -> 2.71 us  [local(): recv = lax.all_to_all(msg.reshape(16, ROWS1, 128), 'sim', 0, 0, tiled=True)]
    unnamed x16 -> x0, local copies, waits for them, and re-layouts: 0.86 us -> none
    pallas_call x1, Pallas kernels: 1.94 us -> 1.18 us  [local(): pl.pallas_call(last_kernel, in_specs=[vmem], out_specs=[vmem] * 3, out_sh...]
  transfers between devices with their start and end apart: 8 -> 5, of which waited for: 5 -> 4; matrix products, arithmetic and copies ran while one was open for 0% -> 0% of each run, Pallas kernels for 0% -> 1%
where the time goes in v2:
time: 44.2 us; the launch traced here: 43.9 us
  starting transfers between devices  12.8 us (29%)
  blocking collectives  12.6 us (29%)
  Pallas kernels  10.1 us (23%)
  waiting for transfers between devices  7.81 us (18%)
  between operations  0.67 us (2%)
    all_to_all x1, blocking collectives, local(): recv2 = lax.all_to_all(msg2.reshape(16, ROWS, 128), 'sim', 0, 0, tiled=True)  12.6 us
    all_to_all x1, starting transfers between devices, local(): recv = lax.all_to_all(msg.reshape(16, ROWS1, 128), 'sim', 0, 0, tiled=True)  8 us
    pallas_call x1, Pallas kernels, local(): pl.pallas_call(tile_kernel, in_specs=[pl.BlockSpec(memory_space=pl.ANY)]...  6.74 us
    ppermute x3, starting transfers between devices, local(): parts.append(lax.ppermute(glob, 'section', pairs))  4.68 us
    ppermute x3, waiting for transfers between devices, local(): parts.append(lax.ppermute(glob, 'section', pairs))  3.93 us
    all_to_all x1, waiting for transfers between devices, local(): recv = lax.all_to_all(msg.reshape(16, ROWS1, 128), 'sim', 0, 0, tiled=True)  2.71 us
    pallas_call x1, Pallas kernels, local(): pl.pallas_call(slab_kernel, in_specs=[smem, smem] + [vmem] * 3, out_specs...  1.83 us
    pallas_call x1, Pallas kernels, local(): pl.pallas_call(last_kernel, in_specs=[vmem], out_specs=[vmem] * 3, out_sh...  1.18 us
  transfers between devices with their start and end apart: 5, of which 4 were waited for; matrix products, arithmetic and copies ran while one was open for 0% of the time, Pallas kernels for 1%

profile of v2, /device:TPU:0, one launch (start us, length us, event | category | flops | bytes accessed | tf_op | source)
XLA Modules:
  0.0 43.9 jit_solution(12380675784376767181)
XLA Ops:
  0.6 6.7 %tile.1 = (f32[1280,128]{1,0:T(8,128)}, f32[24,128]{1,0:T(8,128)S(1)}) custom-call(s32[32]{0:T(128)} %counts.1, f32[32,64,1024]{2,1,0:T(8,128)} %state.1), custom_call_target="tpu_custom_call" | custom-call | tf_op jit(solution)/shard_map/tile/pallas_call | solution.py:251
  7.4 8.0 %all-to-all-start = ((f32[16,80,128]{2,1,0:T(8,128)}), f32[16,80,128]{2,1,0:T(8,128)S(1)}, u32[]{:S(2)}, u32[]{:S(2)}) async-start(f32[16,80,128]{2,1,0:T(8,128)} %bitcast.1), calls=%async_computation | async-start | bytes 1310720 | tf_op jit(solution)/shard_map/slices/all_to_all | solution.py:273
  15.4 3.1 %collective-permute-start.2 = (f32[24,128]{1,0:T(8,128)S(1)}, f32[24,128]{1,0:T(8,128)S(1)}, u32[]{:S(2)}, u32[]{:S(2)}) collective-permute-start(f32[24,128]{1,0:T(8,128)S(1)} %get-tuple-element.14.refs_0_), channel_id=1, source_target_pairs={{0,96},{16,112},{32,0},{48,16},{64,32},{80,48},{96,64},{112,80},{1... | collective-permute-start | bytes 36872 | tf_op jit(solution)/shard_map/along_y3/ppermute | solution.py:278
  18.5 0.6 %collective-permute-start.1 = (f32[24,128]{1,0:T(8,128)S(1)}, f32[24,128]{1,0:T(8,128)S(1)}, u32[]{:S(2)}, u32[]{:S(2)}) collective-permute-start(f32[24,128]{1,0:T(8,128)S(1)} %get-tuple-element.14.refs_0_), channel_id=1, source_target_pairs={{0,64},{16,80},{32,96},{48,112},{64,0},{80,16},{96,32},{112,48},{1... | collective-permute-start | bytes 36872 | tf_op jit(solution)/shard_map/along_y2/ppermute | solution.py:278
  19.1 1.0 %collective-permute-start = (f32[24,128]{1,0:T(8,128)S(1)}, f32[24,128]{1,0:T(8,128)S(1)}, u32[]{:S(2)}, u32[]{:S(2)}) collective-permute-start(f32[24,128]{1,0:T(8,128)S(1)} %get-tuple-element.14.refs_0_), channel_id=1, source_target_pairs={{0,32},{16,48},{32,64},{48,80},{64,96},{80,112},{96,0},{112,16},{1... | collective-permute-start | bytes 36872 | tf_op jit(solution)/shard_map/along_y1/ppermute | solution.py:278
  20.1 0.0 collective-permute-done.2.refs_3_
  20.1 3.6 %collective-permute-done.1.refs_2_ = f32[24,128]{1,0:T(8,128)S(1)} collective-permute-done((f32[24,128]{1,0:T(8,128)S(1)}, f32[24,128]{1,0:T(8,128)S(1)}, u32[]{:S(2)}, u32[]{:S(2)}) %collective-permute-start.1) | collective-permute-done | bytes 12320 | tf_op jit(solution)/shard_map/along_y2/ppermute | solution.py:278
  23.7 0.3 collective-permute-done.refs_1_
  24.0 0.3 merge.1.rest_0_
  24.4 0.1 collective-permute-start.3
  24.5 1.2 %collective-permute-done.3.rest_1_ = f32[24,128]{1,0:T(8,128)S(1)} collective-permute-done((f32[24,128]{1,0:T(8,128)S(1)}, f32[24,128]{1,0:T(8,128)S(1)}, u32[]{:S(2)}, u32[]{:S(2)}) %collective-permute-start.3) | collective-permute-done | bytes 12320 | tf_op jit(solution)/shard_map/cores/ppermute | solution.py:288
  25.6 2.7 %all-to-all-done.recv = f32[16,80,128]{2,1,0:T(8,128)S(1)} async-done(((f32[16,80,128]{2,1,0:T(8,128)}), f32[16,80,128]{2,1,0:T(8,128)S(1)}, u32[]{:S(2)}, u32[]{:S(2)}) %all-to-all-start) | async-done | bytes 655392 | tf_op jit(solution)/shard_map/slices/all_to_all | solution.py:273
  28.3 1.8 %slab.1 = (f32[32,64]{1,0:T(8,128)}, f32[32,256]{1,0:T(8,128)}, f32[384,128]{1,0:T(8,128)S(1)}) custom-call(s32[32]{0:T(128)} %counts.1, s32[32]{0:T(128)} %bitcast.5, f32[16,80,128]{2,1,0:T(8,128)S(1)} %all-to-all-done.recv, f32[24,128]{1,0:T(8,128)S(1)} %merge.1.rest_0_, f32[24,128]{1,0:T(8,128)S(1)} %collective-permute-done.3.rest_1_), custom_call_target="tpu_custom_call" | custom-call | tf_op jit(solution)/shard_map/slab/pallas_call | solution.py:289
  30.2 12.6 %all_to_all.10.recv = f32[16,24,128]{2,1,0:T(8,128)S(1)} all-to-all(f32[16,24,128]{2,1,0:T(8,128)S(1)} %bitcast.4), channel_id=1, replica_groups=mesh['section'=8,'sim'=16] {'sim'}, dimensions={0} | all-to-all | bytes 393216 | tf_op jit(solution)/shard_map/groups/all_to_all | solution.py:303
  42.7 1.2 %last.1 = (f32[1,4096]{1,0:T(1,128)}, f32[1,64]{1,0:T(1,128)}, f32[64,64]{1,0:T(8,128)}) custom-call(f32[16,24,128]{2,1,0:T(8,128)S(1)} %all_to_all.10.recv), custom_call_target="tpu_custom_call" | custom-call | tf_op jit(solution)/shard_map/last/pallas_call | solution.py:304
Async XLA Ops:
  7.4 20.9 %all-to-all-start = ((f32[16,80,128]{2,1,0:T(8,128)}), f32[16,80,128]{2,1,0:T(8,128)S(1)}, u32[]{:S(2)}, u32[]{:S(2)}) async-start(f32[16,80,128]{2,1,0:T(8,128)} %bitcast.1), calls=%async_computation | async-start | bytes 1310720 | tf_op jit(solution)/shard_map/slices/all_to_all | solution.py:273
  15.4 4.7 %collective-permute-start.2 = (f32[24,128]{1,0:T(8,128)S(1)}, f32[24,128]{1,0:T(8,128)S(1)}, u32[]{:S(2)}, u32[]{:S(2)}) collective-permute-start(f32[24,128]{1,0:T(8,128)S(1)} %get-tuple-element.14.refs_0_), channel_id=1, source_target_pairs={{0,96},{16,112},{32,0},{48,16},{64,32},{80,48},{96,64},{112,80},{1... | collective-permute-start | bytes 36872 | tf_op jit(solution)/shard_map/along_y3/ppermute | solution.py:278
  18.5 5.2 %collective-permute-start.1 = (f32[24,128]{1,0:T(8,128)S(1)}, f32[24,128]{1,0:T(8,128)S(1)}, u32[]{:S(2)}, u32[]{:S(2)}) collective-permute-start(f32[24,128]{1,0:T(8,128)S(1)} %get-tuple-element.14.refs_0_), channel_id=1, source_target_pairs={{0,64},{16,80},{32,96},{48,112},{64,0},{80,16},{96,32},{112,48},{1... | collective-permute-start | bytes 36872 | tf_op jit(solution)/shard_map/along_y2/ppermute | solution.py:278
  19.1 4.9 %collective-permute-start = (f32[24,128]{1,0:T(8,128)S(1)}, f32[24,128]{1,0:T(8,128)S(1)}, u32[]{:S(2)}, u32[]{:S(2)}) collective-permute-start(f32[24,128]{1,0:T(8,128)S(1)} %get-tuple-element.14.refs_0_), channel_id=1, source_target_pairs={{0,32},{16,48},{32,64},{48,80},{64,96},{80,112},{96,0},{112,16},{1... | collective-permute-start | bytes 36872 | tf_op jit(solution)/shard_map/along_y1/ppermute | solution.py:278
  24.4 1.3 %collective-permute-start.3 = (f32[24,128]{1,0:T(8,128)S(1)}, f32[24,128]{1,0:T(8,128)S(1)}, u32[]{:S(2)}, u32[]{:S(2)}) collective-permute-start(f32[24,128]{1,0:T(8,128)S(1)} %merge.1.rest_0_), channel_id=1, source_target_pairs={{0,16},{16,0},{32,48},{48,32},{64,80},{80,64},{96,112},{112,96},{1... | collective-permute-start | bytes 36872 | tf_op jit(solution)/shard_map/cores/ppermute | solution.py:288

commit v3 on v2

--- a/solution.py
+++ b/solution.py
@@ -102,14 +102,16 @@
     return pltpu.make_async_copy(state.at[rows], held.at[rows], sems.at[i])
 
 
-def tile_kernel(counts_in, state, msg, glob, counts, held, mids, means, sums, stage, sem, sems):
+def tile_kernel(counts_in, owner_in, state, msg, glob, info, counts, owner, held, mids, means, sums, stage, small, sems):
     first_cell = lax.axis_index("sim") * 1024
     chunks = 32 // CHUNK
     for i in range(chunks):
         copy_in(state, held, sems, i).start()
         if i == 0:
-            counted = pltpu.make_async_copy(counts_in, counts, sem)
+            counted = pltpu.make_async_copy(counts_in, counts, small.at[0])
+            owned = pltpu.make_async_copy(owner_in, owner, small.at[1])
             counted.start()
+            owned.start()
     means[...] = jnp.zeros_like(means)
     sums[...] = jnp.zeros_like(sums)
 
@@ -152,6 +154,12 @@
                 msg[pl.ds(r * 16 + pair, 16, stride=ROWS1), :] = stage[k, pl.ds(r, 16, stride=4), :]
 
     counted.wait()
+    owned.wait()
+    row, lane = iota((16, 128), 0), iota((16, 128), 1)
+    info[:32, :] = spread(lambda s: counts[s].astype(F32), iota((32, 128), 0))
+    info[32:48, :] = spread(lambda s: counts[s].astype(F32), jnp.where(lane < V, row, row + 16))
+    names = spread(lambda s: owner[s].astype(F32), lane)
+    info[48:, :] = ((names == row.astype(F32)) & (lane < 32)).astype(F32)
     copy_in(state, held, sems, 0).wait()
     average(0)
 
@@ -165,7 +173,7 @@
     by_pair = means[...].T[:16]
     for j in range(16):
         msg[ROWS1 * j + MEANS : ROWS1 * j + MEANS + 16, :] = by_pair
-    weight = spread(lambda s: valid(s).astype(F32), iota((32, 128), 0))
+    weight = jnp.clip(info[:32, :] - first_cell.astype(F32), 0.0, 1024.0)
     m = doubled(by_pair)
     number = jnp.sum(weight, axis=0, keepdims=True)
     centre = jnp.sum(weight * m, axis=0, keepdims=True) / jnp.maximum(number, 1.0)
@@ -174,20 +182,13 @@
     put(glob, 0, *packed(acc + swap(acc) + dot(weight * off, off, TN)[:V]), centre, number)
 
 
-def slab_kernel(counts, owner, recv, *rest):
-    globs = rest[:2]
-    slab_mean, slab_cov, msg, stage = rest[2:]
+def slab_kernel(info, recv, one, two, results, msg):
     j = lax.axis_index("sim")
-
-    def count(s):
-        return counts[s].astype(F32)
-
-    acc = recv[0, :64, :]
+    acc = recv[0, :V, :]
     for d in range(1, 16):
-        acc = acc + recv[d, :64, :]
-    lane16 = iota((16, 128), 1)
-    sub16 = iota((16, 128), 0)
-    cnt_p = spread(count, jnp.where(lane16 < V, sub16, sub16 + 16))
+        acc = acc + recv[d, :V, :]
+    cnt_c, cnt_p, member = info[:32, :], info[32:48, :], info[48:, :32]
+    low16 = iota((16, 128), 1) < V
     points = jnp.concatenate([recv[d, MEANS : MEANS + 16, :] for d in range(16)], axis=0)
     weight = jnp.concatenate([jnp.clip(cnt_p - 1024.0 * d, 0.0, 1024.0) for d in range(16)], axis=0)
 
@@ -202,23 +203,16 @@
         pick = 4 * j + r + jnp.where(iota((256, 128), 1) < V, 0, V)
         between = over_tiles(jnp.take_along_axis(weighted, pick, axis=1) * off)
         co.append(acc[16 * r : 16 * r + 16] + between)
-    low16 = lane16 < V
     tiles = []
     for t in range(2):
         a, b = co[2 * t], co[2 * t + 1]
         tiles.append(jnp.concatenate([jnp.where(low16, a, swap(b)), jnp.where(low16, swap(a), b)], axis=0))
-    cnt_c = spread(count, iota((32, 128), 0))
     m = doubled(mean_p)
     for par in range(2):
         rows = slice(16 * par, 16 * par + 16)
-        stage[0, pl.ds(par, 16, stride=2), :] = m[rows]
+        results[0, pl.ds(par, 16, stride=2), :] = m[rows]
         for t in range(2):
-            stage[1 + t, pl.ds(par, 16, stride=2), :] = tiles[t][rows] / (cnt_c[rows] - 1.0)
-    slab_mean[...] = stage[0, :, :64]
-    for t in range(2):
-        slab_cov[:, 128 * t : 128 * t + 128] = stage[1 + t]
-    names = spread(lambda s: owner[s].astype(F32), iota((1, 128), 1))[:, :32]
-    member = (names == iota((16, 32), 0).astype(F32)).astype(F32)
+            results[1 + t, pl.ds(par, 16, stride=2), :] = tiles[t][rows] / (cnt_c[rows] - 1.0)
     sizes = dot(member, cnt_c, NN)
     group_mean = dot(member, cnt_c * m, NN) / jnp.maximum(sizes, 1.0)
     off = m - dot(member, group_mean, TN)
@@ -228,12 +222,15 @@
         pick = 4 * j + 2 * t + jnp.where(iota((32, 128), 1) < V, 0, 1)
         inner = tiles[t] + jnp.take_along_axis(weighted, pick, axis=1) * off
         msg[pl.ds(GROUP + t, 16, stride=ROWS), :] = dot(member, inner, NN) / scale
-    column = merged(globs)
+    column = merged([one, two])
     for d in range(16):
         put(msg, ROWS * d, *column)
 
 
-def last_kernel(recv, group_cov, global_mean, global_cov):
+def last_kernel(recv, results, slab_mean, slab_cov, group_cov, global_mean, global_cov):
+    slab_mean[...] = results[0, :, :V]
+    for t in range(2):
+        slab_cov[:, 128 * t : 128 * t + 128] = results[1 + t]
     rows, diag, centre, number = merged([recv.at[d] for d in range(16)])
     global_cov[...] = (unpacked(rows, diag) / (number - 1.0))[:, :V]
     global_mean[...] = centre[:, :V]
@@ -244,31 +241,33 @@
 
 
 def local(state, owner, counts):
-    smem = pl.BlockSpec(memory_space=pltpu.SMEM)
+    anywhere = pl.BlockSpec(memory_space=pl.ANY)
     vmem = pl.BlockSpec(memory_space=pltpu.VMEM)
     hbm = functools.partial(pltpu.with_memory_space_constraint, memory_space=pltpu.HBM)
-    state, counts, owner = hbm(state), hbm(counts), hbm(owner[:, 0])
-    msg, glob = pl.pallas_call(
+    part = jax.ShapeDtypeStruct((ROWS, 128), F32)
+    msg, glob, info = pl.pallas_call(
         tile_kernel,
-        in_specs=[pl.BlockSpec(memory_space=pl.ANY)] * 2,
-        out_specs=[vmem, vmem],
+        in_specs=[anywhere] * 3,
+        out_specs=[vmem] * 3,
         out_shape=[
             jax.ShapeDtypeStruct((16 * ROWS1, 128), F32),
-            jax.ShapeDtypeStruct((ROWS, 128), F32),
+            part,
+            jax.ShapeDtypeStruct((V, 128), F32),
         ],
         scratch_shapes=[
+            pltpu.SMEM((32,), jnp.int32),
             pltpu.SMEM((32,), jnp.int32),
             pltpu.VMEM((32, V, 1024), F32),
             pltpu.VMEM((32, V, 128), F32),
             pltpu.VMEM((128, 128), F32),
-            pltpu.VMEM((64, 128), F32),
-            pltpu.VMEM((CHUNK // 2, 64, 128), F32),
-            pltpu.SemaphoreType.DMA,
+            pltpu.VMEM((V, 128), F32),
+            pltpu.VMEM((CHUNK // 2, V, 128), F32),
+            pltpu.SemaphoreType.DMA((2,)),
             pltpu.SemaphoreType.DMA((32 // CHUNK,)),
         ],
         compiler_params=pltpu.CompilerParams(vmem_limit_bytes=20 * MIB),
         name="tile",
-    )(counts, state)
+    )(hbm(counts), hbm(owner[:, 0]), hbm(state))
     with jax.named_scope("slices"):
         recv = lax.all_to_all(msg.reshape(16, ROWS1, 128), "sim", 0, 0, tiled=True)
     parts = [glob]
@@ -286,34 +285,34 @@
     )(*parts)
     with jax.named_scope("cores"):
         other = lax.ppermute(four, "section", [(i, i ^ 1) for i in range(8)])
-    slab_mean, slab_cov, msg2 = pl.pallas_call(
+    results, msg2 = pl.pallas_call(
         slab_kernel,
-        in_specs=[smem, smem] + [vmem] * 3,
-        out_specs=[vmem] * 3,
+        in_specs=[vmem] * 4,
+        out_specs=[vmem] * 2,
         out_shape=[
-            jax.ShapeDtypeStruct((32, 64), F32),
-            jax.ShapeDtypeStruct((32, 256), F32),
+            jax.ShapeDtypeStruct((3, 32, 128), F32),
             jax.ShapeDtypeStruct((16 * ROWS, 128), F32),
         ],
-        scratch_shapes=[pltpu.VMEM((3, 32, 128), F32)],
         compiler_params=pltpu.CompilerParams(vmem_limit_bytes=4 * MIB),
         name="slab",
-    )(counts, owner, recv, four, other)
+    )(info, recv, four, other)
     with jax.named_scope("groups"):
         recv2 = lax.all_to_all(msg2.reshape(16, ROWS, 128), "sim", 0, 0, tiled=True)
-    group_cov, global_mean, global_cov = pl.pallas_call(
+    slab_mean, slab_cov, group_cov, global_mean, global_cov = pl.pallas_call(
         last_kernel,
-        in_specs=[vmem],
-        out_specs=[vmem] * 3,
+        in_specs=[vmem] * 2,
+        out_specs=[vmem] * 5,
         out_shape=[
-            jax.ShapeDtypeStruct((1, 4096), F32),
-            jax.ShapeDtypeStruct((1, 64), F32),
-            jax.ShapeDtypeStruct((64, 64), F32),
+            jax.ShapeDtypeStruct((32, V), F32),
+            jax.ShapeDtypeStruct((32, 256), F32),
+            jax.ShapeDtypeStruct((1, V * V), F32),
+            jax.ShapeDtypeStruct((1, V), F32),
+            jax.ShapeDtypeStruct((V, V), F32),
         ],
         compiler_params=pltpu.CompilerParams(vmem_limit_bytes=2 * MIB),
         name="last",
-    )(recv2)
-    return slab_mean, slab_cov, group_cov, global_mean.reshape(64), global_cov
+    )(recv2, results)
+    return slab_mean, slab_cov, group_cov, global_mean.reshape(V), global_cov
 
 
 def solution(mesh):

time: 44.2 us -> 43.1 us (0.975)
  Pallas kernels: 10.1 us -> 9 us
    pallas_call x3, Pallas kernels: 9.76 us -> 8.66 us  [the longest x1 6.67 us: local(): pl.pallas_call(tile_kernel, in_specs=[anywhere] * 3, out_specs=[vmem] * 3...]
where the time goes in v3:
time: 43.1 us; the launch traced here: 42.8 us
  starting transfers between devices  12.8 us (30%)
  blocking collectives  12.6 us (29%)
  Pallas kernels  9 us (21%)
  waiting for transfers between devices  7.81 us (18%)
  between operations  0.68 us (2%)
    all_to_all x1, blocking collectives, local(): recv2 = lax.all_to_all(msg2.reshape(16, ROWS, 128), 'sim', 0, 0, tiled=True)  12.6 us
    all_to_all x1, starting transfers between devices, local(): recv = lax.all_to_all(msg.reshape(16, ROWS1, 128), 'sim', 0, 0, tiled=True)  8 us
    pallas_call x1, Pallas kernels, local(): pl.pallas_call(tile_kernel, in_specs=[anywhere] * 3, out_specs=[vmem] * 3...  6.67 us
    ppermute x3, starting transfers between devices, local(): parts.append(lax.ppermute(glob, 'section', pairs))  4.69 us
    ppermute x3, waiting for transfers between devices, local(): parts.append(lax.ppermute(glob, 'section', pairs))  3.93 us
    all_to_all x1, waiting for transfers between devices, local(): recv = lax.all_to_all(msg.reshape(16, ROWS1, 128), 'sim', 0, 0, tiled=True)  2.71 us
    pallas_call x1, Pallas kernels, local(): pl.pallas_call(last_kernel, in_specs=[vmem] * 2, out_specs=[vmem] * 5, ou...  1.19 us
    ppermute x1, waiting for transfers between devices, local(): other = lax.ppermute(four, 'section', [(i, i ^ 1) for i in range(8)])  1.16 us
  transfers between devices with their start and end apart: 5, of which 4 were waited for; matrix products, arithmetic and copies ran while one was open for 0% of the time, Pallas kernels for 1%

profile of v3, /device:TPU:0, one launch (start us, length us, event | category | flops | bytes accessed | tf_op | source)
XLA Modules:
  0.0 42.8 jit_solution(15467923031477970438)
XLA Ops:
  0.6 6.7 %tile.1 = (f32[1280,128]{1,0:T(8,128)}, f32[24,128]{1,0:T(8,128)S(1)}, f32[64,128]{1,0:T(8,128)S(1)}) custom-call(s32[32]{0:T(128)} %counts_in.1, s32[32]{0:T(128)} %bitcast.5, f32[32,64,1024]{2,1,0:T(8,128)} %state.1), custom_call_target="tpu_custom_call" | custom-call | tf_op jit(solution)/shard_map/tile/pallas_call | solution.py:248
  7.3 8.0 %all-to-all-start = ((f32[16,80,128]{2,1,0:T(8,128)}), f32[16,80,128]{2,1,0:T(8,128)S(1)}, u32[]{:S(2)}, u32[]{:S(2)}) async-start(f32[16,80,128]{2,1,0:T(8,128)} %bitcast.1), calls=%async_computation | async-start | bytes 1310720 | tf_op jit(solution)/shard_map/slices/all_to_all | solution.py:272
  15.3 3.1 %collective-permute-start.2 = (f32[24,128]{1,0:T(8,128)S(1)}, f32[24,128]{1,0:T(8,128)S(1)}, u32[]{:S(2)}, u32[]{:S(2)}) collective-permute-start(f32[24,128]{1,0:T(8,128)S(1)} %get-tuple-element.17.refs_0_), channel_id=1, source_target_pairs={{0,96},{16,112},{32,0},{48,16},{64,32},{80,48},{96,64},{112,80},{1... | collective-permute-start | bytes 36872 | tf_op jit(solution)/shard_map/along_y3/ppermute | solution.py:277
  18.4 0.6 %collective-permute-start.1 = (f32[24,128]{1,0:T(8,128)S(1)}, f32[24,128]{1,0:T(8,128)S(1)}, u32[]{:S(2)}, u32[]{:S(2)}) collective-permute-start(f32[24,128]{1,0:T(8,128)S(1)} %get-tuple-element.17.refs_0_), channel_id=1, source_target_pairs={{0,64},{16,80},{32,96},{48,112},{64,0},{80,16},{96,32},{112,48},{1... | collective-permute-start | bytes 36872 | tf_op jit(solution)/shard_map/along_y2/ppermute | solution.py:277
  19.0 1.0 %collective-permute-start = (f32[24,128]{1,0:T(8,128)S(1)}, f32[24,128]{1,0:T(8,128)S(1)}, u32[]{:S(2)}, u32[]{:S(2)}) collective-permute-start(f32[24,128]{1,0:T(8,128)S(1)} %get-tuple-element.17.refs_0_), channel_id=1, source_target_pairs={{0,32},{16,48},{32,64},{48,80},{64,96},{80,112},{96,0},{112,16},{1... | collective-permute-start | bytes 36872 | tf_op jit(solution)/shard_map/along_y1/ppermute | solution.py:277
  20.0 0.0 collective-permute-done.2.refs_3_
  20.0 3.6 %collective-permute-done.1.refs_2_ = f32[24,128]{1,0:T(8,128)S(1)} collective-permute-done((f32[24,128]{1,0:T(8,128)S(1)}, f32[24,128]{1,0:T(8,128)S(1)}, u32[]{:S(2)}, u32[]{:S(2)}) %collective-permute-start.1) | collective-permute-done | bytes 12320 | tf_op jit(solution)/shard_map/along_y2/ppermute | solution.py:277
  23.6 0.3 collective-permute-done.refs_1_
  23.9 0.3 merge.1.one
  24.3 0.1 collective-permute-start.3
  24.4 1.2 %collective-permute-done.3.two = f32[24,128]{1,0:T(8,128)S(1)} collective-permute-done((f32[24,128]{1,0:T(8,128)S(1)}, f32[24,128]{1,0:T(8,128)S(1)}, u32[]{:S(2)}, u32[]{:S(2)}) %collective-permute-start.3) | collective-permute-done | bytes 12320 | tf_op jit(solution)/shard_map/cores/ppermute | solution.py:287
  25.6 2.7 %all-to-all-done.recv = f32[16,80,128]{2,1,0:T(8,128)S(1)} async-done(((f32[16,80,128]{2,1,0:T(8,128)}), f32[16,80,128]{2,1,0:T(8,128)S(1)}, u32[]{:S(2)}, u32[]{:S(2)}) %all-to-all-start) | async-done | bytes 655392 | tf_op jit(solution)/shard_map/slices/all_to_all | solution.py:272
  28.3 0.8 %slab.1 = (f32[3,32,128]{2,1,0:T(8,128)S(1)}, f32[384,128]{1,0:T(8,128)S(1)}) custom-call(f32[64,128]{1,0:T(8,128)S(1)} %get-tuple-element.15.info, f32[16,80,128]{2,1,0:T(8,128)S(1)} %all-to-all-done.recv, f32[24,128]{1,0:T(8,128)S(1)} %merge.1.one, f32[24,128]{1,0:T(8,128)S(1)} %collective-permute-done.3.two), custom_call_target="tpu_custom_call" | custom-call | tf_op jit(solution)/shard_map/slab/pallas_call | solution.py:288
  29.1 12.6 %all_to_all.10.recv = f32[16,24,128]{2,1,0:T(8,128)S(1)} all-to-all(f32[16,24,128]{2,1,0:T(8,128)S(1)} %bitcast.4), channel_id=1, replica_groups=mesh['section'=8,'sim'=16] {'sim'}, dimensions={0} | all-to-all | bytes 393216 | tf_op jit(solution)/shard_map/groups/all_to_all | solution.py:300
  41.7 1.2 %last.1 = (f32[32,64]{1,0:T(8,128)}, f32[32,256]{1,0:T(8,128)}, f32[1,4096]{1,0:T(1,128)}, f32[1,64]{1,0:T(1,128)}, f32[64,64]{1,0:T(8,128)}) custom-call(f32[16,24,128]{2,1,0:T(8,128)S(1)} %all_to_all.10.recv, f32[3,32,128]{2,1,0:T(8,128)S(1)} %get-tuple-element.19.results), custom_call_target="tpu_custom_call" | custom-call | tf_op jit(solution)/shard_map/last/pallas_call | solution.py:301
Async XLA Ops:
  7.3 20.9 %all-to-all-start = ((f32[16,80,128]{2,1,0:T(8,128)}), f32[16,80,128]{2,1,0:T(8,128)S(1)}, u32[]{:S(2)}, u32[]{:S(2)}) async-start(f32[16,80,128]{2,1,0:T(8,128)} %bitcast.1), calls=%async_computation | async-start | bytes 1310720 | tf_op jit(solution)/shard_map/slices/all_to_all | solution.py:272
  15.3 4.7 %collective-permute-start.2 = (f32[24,128]{1,0:T(8,128)S(1)}, f32[24,128]{1,0:T(8,128)S(1)}, u32[]{:S(2)}, u32[]{:S(2)}) collective-permute-start(f32[24,128]{1,0:T(8,128)S(1)} %get-tuple-element.17.refs_0_), channel_id=1, source_target_pairs={{0,96},{16,112},{32,0},{48,16},{64,32},{80,48},{96,64},{112,80},{1... | collective-permute-start | bytes 36872 | tf_op jit(solution)/shard_map/along_y3/ppermute | solution.py:277
  18.4 5.2 %collective-permute-start.1 = (f32[24,128]{1,0:T(8,128)S(1)}, f32[24,128]{1,0:T(8,128)S(1)}, u32[]{:S(2)}, u32[]{:S(2)}) collective-permute-start(f32[24,128]{1,0:T(8,128)S(1)} %get-tuple-element.17.refs_0_), channel_id=1, source_target_pairs={{0,64},{16,80},{32,96},{48,112},{64,0},{80,16},{96,32},{112,48},{1... | collective-permute-start | bytes 36872 | tf_op jit(solution)/shard_map/along_y2/ppermute | solution.py:277
  19.0 4.9 %collective-permute-start = (f32[24,128]{1,0:T(8,128)S(1)}, f32[24,128]{1,0:T(8,128)S(1)}, u32[]{:S(2)}, u32[]{:S(2)}) collective-permute-start(f32[24,128]{1,0:T(8,128)S(1)} %get-tuple-element.17.refs_0_), channel_id=1, source_target_pairs={{0,32},{16,48},{32,64},{48,80},{64,96},{80,112},{96,0},{112,16},{1... | collective-permute-start | bytes 36872 | tf_op jit(solution)/shard_map/along_y1/ppermute | solution.py:277
  24.3 1.3 %collective-permute-start.3 = (f32[24,128]{1,0:T(8,128)S(1)}, f32[24,128]{1,0:T(8,128)S(1)}, u32[]{:S(2)}, u32[]{:S(2)}) collective-permute-start(f32[24,128]{1,0:T(8,128)S(1)} %merge.1.one), channel_id=1, source_target_pairs={{0,16},{16,0},{32,48},{48,32},{64,80},{80,64},{96,112},{112,96},{1... | collective-permute-start | bytes 36872 | tf_op jit(solution)/shard_map/cores/ppermute | solution.py:287

commit v4 on v3

--- a/solution.py
+++ b/solution.py
@@ -159,7 +159,12 @@
     info[:32, :] = spread(lambda s: counts[s].astype(F32), iota((32, 128), 0))
     info[32:48, :] = spread(lambda s: counts[s].astype(F32), jnp.where(lane < V, row, row + 16))
     names = spread(lambda s: owner[s].astype(F32), lane)
-    info[48:, :] = ((names == row.astype(F32)) & (lane < 32)).astype(F32)
+    member = ((names == row.astype(F32)) & (lane < 32)).astype(F32)
+    weighted = member * spread(lambda s: counts[s].astype(F32), lane)
+    sizes = jnp.sum(weighted, axis=1, keepdims=True)
+    info[48:64, :] = member
+    info[64:80, :] = jnp.broadcast_to(sizes, (16, 128))
+    info[80:, :] = dot(member, weighted / jnp.maximum(sizes, 1.0), TN)[:32]
     copy_in(state, held, sems, 0).wait()
     average(0)
 
@@ -187,7 +192,8 @@
     acc = recv[0, :V, :]
     for d in range(1, 16):
         acc = acc + recv[d, :V, :]
-    cnt_c, cnt_p, member = info[:32, :], info[32:48, :], info[48:, :32]
+    cnt_c, cnt_p, member = info[:32, :], info[32:48, :], info[48:64, :32]
+    sizes, average = info[64:80, :], info[80:, :32]
     low16 = iota((16, 128), 1) < V
     points = jnp.concatenate([recv[d, MEANS : MEANS + 16, :] for d in range(16)], axis=0)
     weight = jnp.concatenate([jnp.clip(cnt_p - 1024.0 * d, 0.0, 1024.0) for d in range(16)], axis=0)
@@ -213,9 +219,7 @@
         results[0, pl.ds(par, 16, stride=2), :] = m[rows]
         for t in range(2):
             results[1 + t, pl.ds(par, 16, stride=2), :] = tiles[t][rows] / (cnt_c[rows] - 1.0)
-    sizes = dot(member, cnt_c, NN)
-    group_mean = dot(member, cnt_c * m, NN) / jnp.maximum(sizes, 1.0)
-    off = m - dot(member, group_mean, TN)
+    off = m - dot(average, m, NN)
     weighted = cnt_c * off
     scale = jnp.maximum(sizes - 1.0, 1.0)
     for t in range(2):
@@ -252,7 +256,7 @@
         out_shape=[
             jax.ShapeDtypeStruct((16 * ROWS1, 128), F32),
             part,
-            jax.ShapeDtypeStruct((V, 128), F32),
+            jax.ShapeDtypeStruct((112, 128), F32),
         ],
         scratch_shapes=[
             pltpu.SMEM((32,), jnp.int32),

time: 43.1 us -> 43 us (level)
  no operation moved by 1% of the time
where the time goes in v4:
time: 43 us; the launch traced here: 42.8 us
  starting transfers between devices  12.8 us (30%)
  blocking collectives  12.6 us (29%)
  Pallas kernels  8.96 us (21%)
  waiting for transfers between devices  7.81 us (18%)
  between operations  0.68 us (2%)
    all_to_all x1, blocking collectives, local(): recv2 = lax.all_to_all(msg2.reshape(16, ROWS, 128), 'sim', 0, 0, tiled=True)  12.6 us
    all_to_all x1, starting transfers between devices, local(): recv = lax.all_to_all(msg.reshape(16, ROWS1, 128), 'sim', 0, 0, tiled=True)  8 us
    pallas_call x1, Pallas kernels, local(): pl.pallas_call(tile_kernel, in_specs=[anywhere] * 3, out_specs=[vmem] * 3...  6.67 us
    ppermute x3, starting transfers between devices, local(): parts.append(lax.ppermute(glob, 'section', pairs))  4.69 us
    ppermute x3, waiting for transfers between devices, local(): parts.append(lax.ppermute(glob, 'section', pairs))  3.93 us
    all_to_all x1, waiting for transfers between devices, local(): recv = lax.all_to_all(msg.reshape(16, ROWS1, 128), 'sim', 0, 0, tiled=True)  2.71 us
    pallas_call x1, Pallas kernels, local(): pl.pallas_call(last_kernel, in_specs=[vmem] * 2, out_specs=[vmem] * 5, ou...  1.18 us
    ppermute x1, waiting for transfers between devices, local(): other = lax.ppermute(four, 'section', [(i, i ^ 1) for i in range(8)])  1.16 us
  transfers between devices with their start and end apart: 5, of which 4 were waited for; matrix products, arithmetic and copies ran while one was open for 0% of the time, Pallas kernels for 1%

profile of v4, /device:TPU:0, one launch (start us, length us, event | category | flops | bytes accessed | tf_op | source)
XLA Modules:
  0.0 42.8 jit_solution(8429279795956522434)
XLA Ops:
  0.6 6.7 %tile.1 = (f32[1280,128]{1,0:T(8,128)}, f32[24,128]{1,0:T(8,128)S(1)}, f32[112,128]{1,0:T(8,128)S(1)}) custom-call(s32[32]{0:T(128)} %counts_in.1, s32[32]{0:T(128)} %bitcast.5, f32[32,64,1024]{2,1,0:T(8,128)} %state.1), custom_call_target="tpu_custom_call" | custom-call | tf_op jit(solution)/shard_map/tile/pallas_call | solution.py:252
  7.3 8.0 %all-to-all-start = ((f32[16,80,128]{2,1,0:T(8,128)}), f32[16,80,128]{2,1,0:T(8,128)S(1)}, u32[]{:S(2)}, u32[]{:S(2)}) async-start(f32[16,80,128]{2,1,0:T(8,128)} %bitcast.1), calls=%async_computation | async-start | bytes 1310720 | tf_op jit(solution)/shard_map/slices/all_to_all | solution.py:276
  15.3 3.1 %collective-permute-start.2 = (f32[24,128]{1,0:T(8,128)S(1)}, f32[24,128]{1,0:T(8,128)S(1)}, u32[]{:S(2)}, u32[]{:S(2)}) collective-permute-start(f32[24,128]{1,0:T(8,128)S(1)} %get-tuple-element.17.refs_0_), channel_id=1, source_target_pairs={{0,96},{16,112},{32,0},{48,16},{64,32},{80,48},{96,64},{112,80},{1... | collective-permute-start | bytes 36872 | tf_op jit(solution)/shard_map/along_y3/ppermute | solution.py:281
  18.4 0.6 %collective-permute-start.1 = (f32[24,128]{1,0:T(8,128)S(1)}, f32[24,128]{1,0:T(8,128)S(1)}, u32[]{:S(2)}, u32[]{:S(2)}) collective-permute-start(f32[24,128]{1,0:T(8,128)S(1)} %get-tuple-element.17.refs_0_), channel_id=1, source_target_pairs={{0,64},{16,80},{32,96},{48,112},{64,0},{80,16},{96,32},{112,48},{1... | collective-permute-start | bytes 36872 | tf_op jit(solution)/shard_map/along_y2/ppermute | solution.py:281
  19.0 1.0 %collective-permute-start = (f32[24,128]{1,0:T(8,128)S(1)}, f32[24,128]{1,0:T(8,128)S(1)}, u32[]{:S(2)}, u32[]{:S(2)}) collective-permute-start(f32[24,128]{1,0:T(8,128)S(1)} %get-tuple-element.17.refs_0_), channel_id=1, source_target_pairs={{0,32},{16,48},{32,64},{48,80},{64,96},{80,112},{96,0},{112,16},{1... | collective-permute-start | bytes 36872 | tf_op jit(solution)/shard_map/along_y1/ppermute | solution.py:281
  20.0 0.0 collective-permute-done.2.refs_3_
  20.0 3.6 %collective-permute-done.1.refs_2_ = f32[24,128]{1,0:T(8,128)S(1)} collective-permute-done((f32[24,128]{1,0:T(8,128)S(1)}, f32[24,128]{1,0:T(8,128)S(1)}, u32[]{:S(2)}, u32[]{:S(2)}) %collective-permute-start.1) | collective-permute-done | bytes 12320 | tf_op jit(solution)/shard_map/along_y2/ppermute | solution.py:281
  23.6 0.3 collective-permute-done.refs_1_
  23.9 0.3 merge.1.one
  24.3 0.1 collective-permute-start.3
  24.4 1.2 %collective-permute-done.3.two = f32[24,128]{1,0:T(8,128)S(1)} collective-permute-done((f32[24,128]{1,0:T(8,128)S(1)}, f32[24,128]{1,0:T(8,128)S(1)}, u32[]{:S(2)}, u32[]{:S(2)}) %collective-permute-start.3) | collective-permute-done | bytes 12320 | tf_op jit(solution)/shard_map/cores/ppermute | solution.py:291
  25.6 2.7 %all-to-all-done.recv = f32[16,80,128]{2,1,0:T(8,128)S(1)} async-done(((f32[16,80,128]{2,1,0:T(8,128)}), f32[16,80,128]{2,1,0:T(8,128)S(1)}, u32[]{:S(2)}, u32[]{:S(2)}) %all-to-all-start) | async-done | bytes 655392 | tf_op jit(solution)/shard_map/slices/all_to_all | solution.py:276
  28.3 0.8 %slab.1 = (f32[3,32,128]{2,1,0:T(8,128)S(1)}, f32[384,128]{1,0:T(8,128)S(1)}) custom-call(f32[112,128]{1,0:T(8,128)S(1)} %get-tuple-element.15.info, f32[16,80,128]{2,1,0:T(8,128)S(1)} %all-to-all-done.recv, f32[24,128]{1,0:T(8,128)S(1)} %merge.1.one, f32[24,128]{1,0:T(8,128)S(1)} %collective-permute-done.3.two), custom_call_target="tpu_custom_call" | custom-call | tf_op jit(solution)/shard_map/slab/pallas_call | solution.py:292
  29.0 12.6 %all_to_all.10.recv = f32[16,24,128]{2,1,0:T(8,128)S(1)} all-to-all(f32[16,24,128]{2,1,0:T(8,128)S(1)} %bitcast.4), channel_id=1, replica_groups=mesh['section'=8,'sim'=16] {'sim'}, dimensions={0} | all-to-all | bytes 393216 | tf_op jit(solution)/shard_map/groups/all_to_all | solution.py:304
  41.6 1.2 %last.1 = (f32[32,64]{1,0:T(8,128)}, f32[32,256]{1,0:T(8,128)}, f32[1,4096]{1,0:T(1,128)}, f32[1,64]{1,0:T(1,128)}, f32[64,64]{1,0:T(8,128)}) custom-call(f32[16,24,128]{2,1,0:T(8,128)S(1)} %all_to_all.10.recv, f32[3,32,128]{2,1,0:T(8,128)S(1)} %get-tuple-element.19.results), custom_call_target="tpu_custom_call" | custom-call | tf_op jit(solution)/shard_map/last/pallas_call | solution.py:305
Async XLA Ops:
  7.3 21.0 %all-to-all-start = ((f32[16,80,128]{2,1,0:T(8,128)}), f32[16,80,128]{2,1,0:T(8,128)S(1)}, u32[]{:S(2)}, u32[]{:S(2)}) async-start(f32[16,80,128]{2,1,0:T(8,128)} %bitcast.1), calls=%async_computation | async-start | bytes 1310720 | tf_op jit(solution)/shard_map/slices/all_to_all | solution.py:276
  15.3 4.7 %collective-permute-start.2 = (f32[24,128]{1,0:T(8,128)S(1)}, f32[24,128]{1,0:T(8,128)S(1)}, u32[]{:S(2)}, u32[]{:S(2)}) collective-permute-start(f32[24,128]{1,0:T(8,128)S(1)} %get-tuple-element.17.refs_0_), channel_id=1, source_target_pairs={{0,96},{16,112},{32,0},{48,16},{64,32},{80,48},{96,64},{112,80},{1... | collective-permute-start | bytes 36872 | tf_op jit(solution)/shard_map/along_y3/ppermute | solution.py:281
  18.4 5.2 %collective-permute-start.1 = (f32[24,128]{1,0:T(8,128)S(1)}, f32[24,128]{1,0:T(8,128)S(1)}, u32[]{:S(2)}, u32[]{:S(2)}) collective-permute-start(f32[24,128]{1,0:T(8,128)S(1)} %get-tuple-element.17.refs_0_), channel_id=1, source_target_pairs={{0,64},{16,80},{32,96},{48,112},{64,0},{80,16},{96,32},{112,48},{1... | collective-permute-start | bytes 36872 | tf_op jit(solution)/shard_map/along_y2/ppermute | solution.py:281
  19.0 4.9 %collective-permute-start = (f32[24,128]{1,0:T(8,128)S(1)}, f32[24,128]{1,0:T(8,128)S(1)}, u32[]{:S(2)}, u32[]{:S(2)}) collective-permute-start(f32[24,128]{1,0:T(8,128)S(1)} %get-tuple-element.17.refs_0_), channel_id=1, source_target_pairs={{0,32},{16,48},{32,64},{48,80},{64,96},{80,112},{96,0},{112,16},{1... | collective-permute-start | bytes 36872 | tf_op jit(solution)/shard_map/along_y1/ppermute | solution.py:281
  24.3 1.3 %collective-permute-start.3 = (f32[24,128]{1,0:T(8,128)S(1)}, f32[24,128]{1,0:T(8,128)S(1)}, u32[]{:S(2)}, u32[]{:S(2)}) collective-permute-start(f32[24,128]{1,0:T(8,128)S(1)} %merge.1.one), channel_id=1, source_target_pairs={{0,16},{16,0},{32,48},{48,32},{64,80},{80,64},{96,112},{112,96},{1... | collective-permute-start | bytes 36872 | tf_op jit(solution)/shard_map/cores/ppermute | solution.py:291

commit v5 on v4

--- a/solution.py
+++ b/solution.py
@@ -187,7 +187,7 @@
     put(glob, 0, *packed(acc + swap(acc) + dot(weight * off, off, TN)[:V]), centre, number)
 
 
-def slab_kernel(info, recv, one, two, results, msg):
+def slab_kernel(info, recv, one, two, three, four, results, msg):
     j = lax.axis_index("sim")
     acc = recv[0, :V, :]
     for d in range(1, 16):
@@ -226,7 +226,7 @@
         pick = 4 * j + 2 * t + jnp.where(iota((32, 128), 1) < V, 0, 1)
         inner = tiles[t] + jnp.take_along_axis(weighted, pick, axis=1) * off
         msg[pl.ds(GROUP + t, 16, stride=ROWS), :] = dot(member, inner, NN) / scale
-    column = merged([one, two])
+    column = merged([one, two, three, four])
     for d in range(16):
         put(msg, ROWS * d, *column)
 
@@ -274,24 +274,24 @@
     )(hbm(counts), hbm(owner[:, 0]), hbm(state))
     with jax.named_scope("slices"):
         recv = lax.all_to_all(msg.reshape(16, ROWS1, 128), "sim", 0, 0, tiled=True)
-    parts = [glob]
+    with jax.named_scope("cores"):
+        other = lax.ppermute(glob, "section", [(i, i ^ 1) for i in range(8)])
+    chip = pl.pallas_call(
+        merge_kernel,
+        in_specs=[vmem] * 2,
+        out_specs=vmem,
+        out_shape=part,
+        compiler_params=pltpu.CompilerParams(vmem_limit_bytes=2 * MIB),
+        name="merge",
+    )(glob, other)
+    parts = [chip]
     for k in range(1, 4):
         with jax.named_scope(f"along_y{k}"):
             pairs = [(i, (i + 2 * k) % 8) for i in range(8)]
-            parts.append(lax.ppermute(glob, "section", pairs))
-    four = pl.pallas_call(
-        merge_kernel,
-        in_specs=[vmem] * 4,
-        out_specs=vmem,
-        out_shape=jax.ShapeDtypeStruct((ROWS, 128), F32),
-        compiler_params=pltpu.CompilerParams(vmem_limit_bytes=2 * MIB),
-        name="merge",
-    )(*parts)
-    with jax.named_scope("cores"):
-        other = lax.ppermute(four, "section", [(i, i ^ 1) for i in range(8)])
+            parts.append(lax.ppermute(chip, "section", pairs))
     results, msg2 = pl.pallas_call(
         slab_kernel,
-        in_specs=[vmem] * 4,
+        in_specs=[vmem] * 6,
         out_specs=[vmem] * 2,
         out_shape=[
             jax.ShapeDtypeStruct((3, 32, 128), F32),
@@ -299,7 +299,7 @@
         ],
         compiler_params=pltpu.CompilerParams(vmem_limit_bytes=4 * MIB),
         name="slab",
-    )(info, recv, four, other)
+    )(info, recv, *parts)
     with jax.named_scope("groups"):
         recv2 = lax.all_to_all(msg2.reshape(16, ROWS, 128), "sim", 0, 0, tiled=True)
     slab_mean, slab_cov, group_cov, global_mean, global_cov = pl.pallas_call(

time: 43 us -> 43 us (level)
  no operation moved by 1% of the time
where the time goes in v5:
time: 43 us; the launch traced here: 42.8 us
  starting transfers between devices  12.8 us (30%)
  blocking collectives  12.6 us (29%)
  Pallas kernels  8.96 us (21%)
  waiting for transfers between devices  7.81 us (18%)
  between operations  0.68 us (2%)
    all_to_all x1, blocking collectives, local(): recv2 = lax.all_to_all(msg2.reshape(16, ROWS, 128), 'sim', 0, 0, tiled=True)  12.6 us
    all_to_all x1, starting transfers between devices, local(): recv = lax.all_to_all(msg.reshape(16, ROWS1, 128), 'sim', 0, 0, tiled=True)  8 us
    pallas_call x1, Pallas kernels, local(): pl.pallas_call(tile_kernel, in_specs=[anywhere] * 3, out_specs=[vmem] * 3...  6.67 us
    ppermute x3, starting transfers between devices, local(): parts.append(lax.ppermute(chip, 'section', pairs))  4.69 us
    ppermute x3, waiting for transfers between devices, local(): parts.append(lax.ppermute(chip, 'section', pairs))  3.93 us
    all_to_all x1, waiting for transfers between devices, local(): recv = lax.all_to_all(msg.reshape(16, ROWS1, 128), 'sim', 0, 0, tiled=True)  2.71 us
    pallas_call x1, Pallas kernels, local(): pl.pallas_call(last_kernel, in_specs=[vmem] * 2, out_specs=[vmem] * 5, ou...  1.19 us
    ppermute x1, waiting for transfers between devices, local(): other = lax.ppermute(glob, 'section', [(i, i ^ 1) for i in range(8)])  1.16 us
  transfers between devices with their start and end apart: 5, of which 4 were waited for; matrix products, arithmetic and copies ran while one was open for 0% of the time, Pallas kernels for 1%

profile of v5, /device:TPU:0, one launch (start us, length us, event | category | flops | bytes accessed | tf_op | source)
XLA Modules:
  0.0 42.8 jit_solution(3547898383481449804)
XLA Ops:
  0.6 6.7 %tile.1 = (f32[1280,128]{1,0:T(8,128)}, f32[24,128]{1,0:T(8,128)S(1)}, f32[112,128]{1,0:T(8,128)S(1)}) custom-call(s32[32]{0:T(128)} %counts_in.1, s32[32]{0:T(128)} %bitcast.5, f32[32,64,1024]{2,1,0:T(8,128)} %state.1), custom_call_target="tpu_custom_call" | custom-call | tf_op jit(solution)/shard_map/tile/pallas_call | solution.py:252
  7.3 8.0 %all-to-all-start = ((f32[16,80,128]{2,1,0:T(8,128)}), f32[16,80,128]{2,1,0:T(8,128)S(1)}, u32[]{:S(2)}, u32[]{:S(2)}) async-start(f32[16,80,128]{2,1,0:T(8,128)} %bitcast.1), calls=%async_computation | async-start | bytes 1310720 | tf_op jit(solution)/shard_map/slices/all_to_all | solution.py:276
  15.3 0.1 collective-permute-start
  15.4 1.2 %collective-permute-done.refs_1_ = f32[24,128]{1,0:T(8,128)S(1)} collective-permute-done((f32[24,128]{1,0:T(8,128)S(1)}, f32[24,128]{1,0:T(8,128)S(1)}, u32[]{:S(2)}, u32[]{:S(2)}) %collective-permute-start) | collective-permute-done | bytes 12320 | tf_op jit(solution)/shard_map/cores/ppermute | solution.py:278
  16.6 0.3 merge.1.one
  16.9 3.1 %collective-permute-start.3 = (f32[24,128]{1,0:T(8,128)S(1)}, f32[24,128]{1,0:T(8,128)S(1)}, u32[]{:S(2)}, u32[]{:S(2)}) collective-permute-start(f32[24,128]{1,0:T(8,128)S(1)} %merge.1.one), channel_id=1, source_target_pairs={{0,96},{16,112},{32,0},{48,16},{64,32},{80,48},{96,64},{112,80},{1... | collective-permute-start | bytes 36872 | tf_op jit(solution)/shard_map/along_y3/ppermute | solution.py:291
  20.0 0.6 %collective-permute-start.2 = (f32[24,128]{1,0:T(8,128)S(1)}, f32[24,128]{1,0:T(8,128)S(1)}, u32[]{:S(2)}, u32[]{:S(2)}) collective-permute-start(f32[24,128]{1,0:T(8,128)S(1)} %merge.1.one), channel_id=1, source_target_pairs={{0,64},{16,80},{32,96},{48,112},{64,0},{80,16},{96,32},{112,48},{1... | collective-permute-start | bytes 36872 | tf_op jit(solution)/shard_map/along_y2/ppermute | solution.py:291
  20.6 1.0 %collective-permute-start.1 = (f32[24,128]{1,0:T(8,128)S(1)}, f32[24,128]{1,0:T(8,128)S(1)}, u32[]{:S(2)}, u32[]{:S(2)}) collective-permute-start(f32[24,128]{1,0:T(8,128)S(1)} %merge.1.one), channel_id=1, source_target_pairs={{0,32},{16,48},{32,64},{48,80},{64,96},{80,112},{96,0},{112,16},{1... | collective-permute-start | bytes 36872 | tf_op jit(solution)/shard_map/along_y1/ppermute | solution.py:291
  21.6 0.0 collective-permute-done.3.four
  21.6 3.6 %collective-permute-done.2.three = f32[24,128]{1,0:T(8,128)S(1)} collective-permute-done((f32[24,128]{1,0:T(8,128)S(1)}, f32[24,128]{1,0:T(8,128)S(1)}, u32[]{:S(2)}, u32[]{:S(2)}) %collective-permute-start.2) | collective-permute-done | bytes 12320 | tf_op jit(solution)/shard_map/along_y2/ppermute | solution.py:291
  25.2 0.3 collective-permute-done.1.two
  25.6 2.7 %all-to-all-done.recv = f32[16,80,128]{2,1,0:T(8,128)S(1)} async-done(((f32[16,80,128]{2,1,0:T(8,128)}), f32[16,80,128]{2,1,0:T(8,128)S(1)}, u32[]{:S(2)}, u32[]{:S(2)}) %all-to-all-start) | async-done | bytes 655392 | tf_op jit(solution)/shard_map/slices/all_to_all | solution.py:276
  28.3 0.8 %slab.1 = (f32[3,32,128]{2,1,0:T(8,128)S(1)}, f32[384,128]{1,0:T(8,128)S(1)}) custom-call(f32[112,128]{1,0:T(8,128)S(1)} %get-tuple-element.15.info, f32[16,80,128]{2,1,0:T(8,128)S(1)} %all-to-all-done.recv, f32[24,128]{1,0:T(8,128)S(1)} %merge.1.one, f32[24,128]{1,0:T(8,128)S(1)} %collective-permute-done.1.two, f32[24,128]{1,0:T(8,128)S(1)} %collective-permute-done.2.three, ...), custom_call_target="tpu_custom_call" | custom-call | tf_op jit(solution)/shard_map/slab/pallas_call | solution.py:292
  29.0 12.6 %all_to_all.10.recv = f32[16,24,128]{2,1,0:T(8,128)S(1)} all-to-all(f32[16,24,128]{2,1,0:T(8,128)S(1)} %bitcast.4), channel_id=1, replica_groups=mesh['section'=8,'sim'=16] {'sim'}, dimensions={0} | all-to-all | bytes 393216 | tf_op jit(solution)/shard_map/groups/all_to_all | solution.py:304
  41.6 1.2 %last.1 = (f32[32,64]{1,0:T(8,128)}, f32[32,256]{1,0:T(8,128)}, f32[1,4096]{1,0:T(1,128)}, f32[1,64]{1,0:T(1,128)}, f32[64,64]{1,0:T(8,128)}) custom-call(f32[16,24,128]{2,1,0:T(8,128)S(1)} %all_to_all.10.recv, f32[3,32,128]{2,1,0:T(8,128)S(1)} %get-tuple-element.19.results), custom_call_target="tpu_custom_call" | custom-call | tf_op jit(solution)/shard_map/last/pallas_call | solution.py:305
Async XLA Ops:
  7.3 21.0 %all-to-all-start = ((f32[16,80,128]{2,1,0:T(8,128)}), f32[16,80,128]{2,1,0:T(8,128)S(1)}, u32[]{:S(2)}, u32[]{:S(2)}) async-start(f32[16,80,128]{2,1,0:T(8,128)} %bitcast.1), calls=%async_computation | async-start | bytes 1310720 | tf_op jit(solution)/shard_map/slices/all_to_all | solution.py:276
  15.3 1.3 %collective-permute-start = (f32[24,128]{1,0:T(8,128)S(1)}, f32[24,128]{1,0:T(8,128)S(1)}, u32[]{:S(2)}, u32[]{:S(2)}) collective-permute-start(f32[24,128]{1,0:T(8,128)S(1)} %get-tuple-element.17.refs_0_), channel_id=1, source_target_pairs={{0,16},{16,0},{32,48},{48,32},{64,80},{80,64},{96,112},{112,96},{1... | collective-permute-start | bytes 36872 | tf_op jit(solution)/shard_map/cores/ppermute | solution.py:278
  16.9 4.7 %collective-permute-start.3 = (f32[24,128]{1,0:T(8,128)S(1)}, f32[24,128]{1,0:T(8,128)S(1)}, u32[]{:S(2)}, u32[]{:S(2)}) collective-permute-start(f32[24,128]{1,0:T(8,128)S(1)} %merge.1.one), channel_id=1, source_target_pairs={{0,96},{16,112},{32,0},{48,16},{64,32},{80,48},{96,64},{112,80},{1... | collective-permute-start | bytes 36872 | tf_op jit(solution)/shard_map/along_y3/ppermute | solution.py:291
  20.0 5.2 %collective-permute-start.2 = (f32[24,128]{1,0:T(8,128)S(1)}, f32[24,128]{1,0:T(8,128)S(1)}, u32[]{:S(2)}, u32[]{:S(2)}) collective-permute-start(f32[24,128]{1,0:T(8,128)S(1)} %merge.1.one), channel_id=1, source_target_pairs={{0,64},{16,80},{32,96},{48,112},{64,0},{80,16},{96,32},{112,48},{1... | collective-permute-start | bytes 36872 | tf_op jit(solution)/shard_map/along_y2/ppermute | solution.py:291
  20.6 4.9 %collective-permute-start.1 = (f32[24,128]{1,0:T(8,128)S(1)}, f32[24,128]{1,0:T(8,128)S(1)}, u32[]{:S(2)}, u32[]{:S(2)}) collective-permute-start(f32[24,128]{1,0:T(8,128)S(1)} %merge.1.one), channel_id=1, source_target_pairs={{0,32},{16,48},{32,64},{48,80},{64,96},{80,112},{96,0},{112,16},{1... | collective-permute-start | bytes 36872 | tf_op jit(solution)/shard_map/along_y1/ppermute | solution.py:291
